TPU v7x, 8 devices: a whole 2x2x1 slice. The times are simulated.
8 devices in a mesh: grp: 1 (over z), comp: 2 (over y), row: 4 (over x, core).
Axes of the slice: x: 2, y: 2, z: 1, core: 2. Of those that a mesh axis runs over, the one named last changes fastest.
Arguments:
- points: bfloat16 [4096, 256], P(('grp', 'row'))
- mu_init: float32 [2, 1024, 128], P(None, ('grp', 'comp'))
- logpi_init: float32 [2, 1024], P(None, ('grp', 'comp'))
- inv_temp: float32 [3], replicated
Outputs:
- output 1: float32 [2, 1024, 128], P(None, ('grp', 'comp'))
- output 2: float32 [2, 1024], P(None, ('grp', 'comp'))
- output 3: float32 [2, 4096], P(None, ('grp', 'row'))
All inputs are finite; a program needn't handle non-finite values.
Results may differ from a plain program's by a relative error of at most 0.00163705.
Values are sent between devices in bfloat16 or wider.
A program may use at most 1 GiB of HBM per device.

v0:
```python
import jax
import jax.numpy as jnp
from jax import lax
from jax.sharding import PartitionSpec as P

EPS_COUNT = 1e-6
PRIOR_ALPHA = 1e-3


def solution(mesh):
    comp_size = mesh.shape["comp"]
    row_size = mesh.shape["row"]

    def local_fit(x_local, mu_init, logpi_init, inv_temp):
        n_rows, full_dim = x_local.shape
        half_dim = full_dim // 2
        n_local = mu_init.shape[1]
        total_pts = n_rows * row_size
        total_comp = n_local * comp_size
        x_fits = jnp.transpose(x_local.reshape(n_rows, 2, half_dim), (1, 0, 2))
        sq_norm = jnp.sum(jnp.square(x_fits.astype(jnp.float32)), axis=2)
        mean_vecs = mu_init
        log_wts = logpi_init
        for sweep_idx in range(inv_temp.shape[0]):
            beta_t = inv_temp[sweep_idx]
            mu_sq = jnp.sum(mean_vecs * mean_vecs, axis=2)
            cross_dot = jnp.einsum("snh,skh->snk", x_fits, mean_vecs.astype(jnp.bfloat16), preferred_element_type=jnp.float32)
            logits = log_wts[:, None, :] - beta_t * (sq_norm[:, :, None] - 2.0 * cross_dot + mu_sq[:, None, :])
            row_max = lax.pmax(jnp.max(logits, axis=2), "comp")
            shifted = jnp.exp(logits - row_max[:, :, None])
            row_sum = lax.psum(jnp.sum(shifted, axis=2), "comp")
            log_norm = row_max + jnp.log(row_sum)
            resp_f = shifted / row_sum[:, :, None]
            counts = jnp.sum(resp_f, axis=1)
            stat_sum = jnp.einsum("snk,snh->skh", resp_f.astype(jnp.bfloat16), x_fits, preferred_element_type=jnp.float32)
            counts, stat_sum = lax.psum((counts, stat_sum), "row")
            mean_vecs = stat_sum / (counts[:, :, None] + EPS_COUNT)
            log_wts = jnp.log((counts + PRIOR_ALPHA) / (total_pts + total_comp * PRIOR_ALPHA))
        return mean_vecs, log_wts, log_norm

    return jax.shard_map(
        local_fit,
        mesh=mesh,
        in_specs=(P(("grp", "row"), None), P(None, ("grp", "comp"), None), P(None, ("grp", "comp")), P()),
        out_specs=(P(None, ("grp", "comp"), None), P(None, ("grp", "comp")), P(None, ("grp", "row"))),
        check_vma=False,
    )
```

profile of v0, /device:TPU:0, one launch (start us, length us, event | category | flops | bytes accessed | tf_op | source)
XLA Modules:
  0.0 179.1 jit_solution(2824271891957946939)
XLA Ops:
  10.2 4.7 %fusion.30 = (f32[2,1024]{1,0:T(2,128)S(1)}, f32[2,1024,512]{1,2,0:T(8,128)}) fusion(f32[2,512]{1,0:T(2,128)S(1)} %multiply_reduce_fusion.3, f32[2,512,128]{2,1,0:T(8,128)} %param.5, f32[2,1024]{1,0:T(2,128)S(1)} %multiply_reduce_fusion, f32[]{:T(128)} %bitcast, f32[2,512]{1,0:T(2,128)} %param.6, bf16[1024,256]{1,0:T(8,128)(2,1)S(1)} %copy-done), kind=kOutput, calls=%fused_computation.50 | convolution fusion | flops 274855936 | bytes 5267460 | tf_op jit(solution)/shard_map/snh,skh->snk/dot_general | solution.py:27
  14.9 6.3 %pmax.21 = f32[2,1024]{1,0:T(2,128)S(1)} all-reduce(f32[2,1024]{1,0:T(2,128)S(1)} %get-tuple-element.12), channel_id=1, replica_groups=mesh['grp'=1,'comp'=2,'row'=4] {'comp'}, use_global_device_ids=true, to_apply=%region_3.0 | all-reduce | flops 2048 | bytes 16384 | tf_op jit(solution)/shard_map/pmax | solution.py:29
  21.2 2.8 %fusion.3 = f32[2,1024]{1,0:T(2,128)S(1)} fusion(f32[2,1024,512]{1,2,0:T(8,128)} %get-tuple-element.13, f32[2,1024]{1,0:T(2,128)S(1)} %pmax.21), kind=kLoop, calls=%fused_computation.11 | loop fusion | flops 2095104 | bytes 4210688 | tf_op jit(solution)/shard_map/reduce_sum | solution.py:31
  24.0 5.0 %psum.63 = f32[2,1024]{1,0:T(2,128)S(1)} all-reduce(f32[2,1024]{1,0:T(2,128)S(1)} %fusion.3), channel_id=1, replica_groups=mesh['grp'=1,'comp'=2,'row'=4] {'comp'}, use_global_device_ids=true, to_apply=%region_5.0 | all-reduce | flops 2048 | bytes 16384 | tf_op jit(solution)/shard_map/psum | solution.py:31
  29.0 3.8 %fusion.12 = f32[2,512,128]{2,1,0:T(8,128)} fusion(f32[2,1024,512]{1,2,0:T(8,128)} %get-tuple-element.13, f32[2,1024]{1,0:T(2,128)S(1)} %psum.63, f32[2,1024]{1,0:T(2,128)S(1)} %pmax.21, bf16[1024,256]{1,0:T(8,128)(2,1)S(1)} %copy-done), kind=kOutput, calls=%fused_computation.20 | convolution fusion | flops 271581184 | bytes 5259264 | tf_op jit(solution)/shard_map/snk,snh->skh/dot_general | solution.py:35
  32.8 3.0 %fusion.19 = f32[2,512]{1,0:T(2,128)S(1)} fusion(f32[2,1024]{1,0:T(2,128)S(1)} %psum.63, f32[2,1024,512]{1,2,0:T(8,128)} %get-tuple-element.13, f32[2,1024]{1,0:T(2,128)S(1)} %pmax.21), kind=kLoop, calls=%fused_computation.24 | loop fusion | flops 3144704 | bytes 4214784 | tf_op jit(solution)/shard_map/reduce_sum | solution.py:34
  35.8 6.2 %psum.64 = f32[2,512]{1,0:T(2,128)S(1)} all-reduce(f32[2,512]{1,0:T(2,128)S(1)} %fusion.19), channel_id=1, replica_groups=mesh['grp'=1,'comp'=2,'row'=4] {'row'}, use_global_device_ids=true, to_apply=%region_7.0 | all-reduce | flops 1024 | bytes 8192 | tf_op jit(solution)/shard_map/psum | solution.py:36
  42.0 20.2 %all-reduce.4.cloned.1.call-done = f32[2,512,128]{2,1,0:T(8,128)} async-done(((f32[2,512,128]{2,1,0:T(8,128)}), f32[2,512,128]{2,1,0:T(8,128)}) %all-reduce.4.cloned.1.call-update) | async-done | bytes 524304 | tf_op jit(solution)/shard_map/psum | solution.py:36
  63.6 4.6 %bitcast_reduce_fusion.1 = (f32[2,1024]{1,0:T(2,128)S(1)}, f32[2,512,1024]{2,1,0:T(8,128)}) fusion(f32[2,512]{1,0:T(2,128)S(1)} %multiply_reduce_fusion.2, f32[2,512,128]{2,1,0:T(8,128)} %all-reduce.4.cloned.1.call-done, f32[2,512]{1,0:T(2,128)S(1)} %get-tuple-element.7, f32[2,1024]{1,0:T(2,128)S(1)} %multiply_reduce_fusion, f32[]{:T(128)} %bitcast.2, ...), kind=kOutput, calls=%fused_computation.4 | convolution fusion | flops 274987008 | bytes 5271556 | tf_op jit(solution)/shard_map/snh,skh->snk/dot_general | solution.py:27
  68.2 5.0 %pmax.22 = f32[2,1024]{1,0:T(2,128)S(1)} all-reduce(f32[2,1024]{1,0:T(2,128)S(1)} %get-tuple-element.14), channel_id=1, replica_groups=mesh['grp'=1,'comp'=2,'row'=4] {'comp'}, use_global_device_ids=true, to_apply=%region_11.0 | all-reduce | flops 2048 | bytes 16384 | tf_op jit(solution)/shard_map/pmax | solution.py:29
  73.2 2.8 %fusion.5 = f32[2,1024]{1,0:T(2,128)S(1)} fusion(f32[2,512,1024]{2,1,0:T(8,128)} %get-tuple-element.15, f32[2,1024]{1,0:T(2,128)S(1)} %pmax.22), kind=kLoop, calls=%fused_computation.13 | loop fusion | flops 2095104 | bytes 4210688 | tf_op jit(solution)/shard_map/reduce_sum | solution.py:31
  75.9 5.0 %psum.66 = f32[2,1024]{1,0:T(2,128)S(1)} all-reduce(f32[2,1024]{1,0:T(2,128)S(1)} %fusion.5), channel_id=1, replica_groups=mesh['grp'=1,'comp'=2,'row'=4] {'comp'}, use_global_device_ids=true, to_apply=%region_13.0 | all-reduce | flops 2048 | bytes 16384 | tf_op jit(solution)/shard_map/psum | solution.py:31
  80.9 3.8 %fusion.10 = f32[2,512,128]{2,1,0:T(8,128)} fusion(f32[2,512,1024]{2,1,0:T(8,128)} %get-tuple-element.15, f32[2,1024]{1,0:T(2,128)S(1)} %psum.66, f32[2,1024]{1,0:T(2,128)S(1)} %pmax.22, bf16[1024,256]{1,0:T(8,128)(2,1)S(1)} %copy-done), kind=kOutput, calls=%fused_computation.18 | convolution fusion | flops 271581184 | bytes 5259264 | tf_op jit(solution)/shard_map/snk,snh->skh/dot_general | solution.py:35
  84.8 3.0 %fusion.17 = f32[2,512]{1,0:T(2,128)S(1)} fusion(f32[2,1024]{1,0:T(2,128)S(1)} %psum.66, f32[2,1024]{1,0:T(2,128)S(1)} %pmax.22, f32[2,512,1024]{2,1,0:T(8,128)} %get-tuple-element.15), kind=kLoop, calls=%fused_computation.23 | loop fusion | flops 3144704 | bytes 4214784 | tf_op jit(solution)/shard_map/reduce_sum | solution.py:34
  87.7 5.8 %psum.67 = f32[2,512]{1,0:T(2,128)S(1)} all-reduce(f32[2,512]{1,0:T(2,128)S(1)} %fusion.17), channel_id=1, replica_groups=mesh['grp'=1,'comp'=2,'row'=4] {'row'}, use_global_device_ids=true, to_apply=%region_15.0 | all-reduce | flops 1024 | bytes 8192 | tf_op jit(solution)/shard_map/psum | solution.py:36
  93.5 19.2 %all-reduce.6.cloned.1.call-done = f32[2,512,128]{2,1,0:T(8,128)} async-done(((f32[2,512,128]{2,1,0:T(8,128)}), f32[2,512,128]{2,1,0:T(8,128)}) %all-reduce.6.cloned.1.call-update) | async-done | bytes 524304 | tf_op jit(solution)/shard_map/psum | solution.py:36
  114.1 4.7 %bitcast_reduce_fusion = (f32[2,1024]{1,0:T(2,128)S(1)}, f32[2,512,1024]{2,1,0:T(8,128)}) fusion(f32[2,512]{1,0:T(2,128)S(1)} %multiply_reduce_fusion.1, f32[2,512,128]{2,1,0:T(8,128)} %all-reduce.6.cloned.1.call-done, f32[2,512]{1,0:T(2,128)S(1)} %get-tuple-element.5, f32[2,1024]{1,0:T(2,128)S(1)} %multiply_reduce_fusion, f32[]{:T(128)} %bitcast.4, ...), kind=kOutput, calls=%fused_computation.1 | convolution fusion | flops 274987008 | bytes 5271556 | tf_op jit(solution)/shard_map/snh,skh->snk/dot_general | solution.py:27
  118.8 5.0 %pmax.23 = f32[2,1024]{1,0:T(2,128)S(1)} all-reduce(f32[2,1024]{1,0:T(2,128)S(1)} %get-tuple-element.16), channel_id=1, replica_groups=mesh['grp'=1,'comp'=2,'row'=4] {'comp'}, use_global_device_ids=true, to_apply=%region_19.0 | all-reduce | flops 2048 | bytes 16384 | tf_op jit(solution)/shard_map/pmax | solution.py:29
  123.8 2.8 %fusion.7 = f32[2,1024]{1,0:T(2,128)S(1)} fusion(f32[2,512,1024]{2,1,0:T(8,128)} %get-tuple-element.17, f32[2,1024]{1,0:T(2,128)S(1)} %pmax.23), kind=kLoop, calls=%fused_computation.15 | loop fusion | flops 2095104 | bytes 4210688 | tf_op jit(solution)/shard_map/reduce_sum | solution.py:31
  126.5 5.0 %psum.69 = f32[2,1024]{1,0:T(2,128)S(1)} all-reduce(f32[2,1024]{1,0:T(2,128)S(1)} %fusion.7), channel_id=1, replica_groups=mesh['grp'=1,'comp'=2,'row'=4] {'comp'}, use_global_device_ids=true, to_apply=%region_21.0 | all-reduce | flops 2048 | bytes 16384 | tf_op jit(solution)/shard_map/psum | solution.py:31
  131.5 3.1 %fusion.14 = f32[2,512]{1,0:T(2,128)S(1)} fusion(f32[2,1024]{1,0:T(2,128)S(1)} %psum.69, f32[2,1024]{1,0:T(2,128)S(1)} %pmax.23, f32[2,512,1024]{2,1,0:T(8,128)} %get-tuple-element.17), kind=kLoop, calls=%fused_computation.22 | loop fusion | flops 3144704 | bytes 4214784 | tf_op jit(solution)/shard_map/reduce_sum | solution.py:34
  136.6 5.7 %psum.71 = f32[2,512]{1,0:T(2,128)S(1)} all-reduce(f32[2,512]{1,0:T(2,128)S(1)} %fusion.14), channel_id=1, replica_groups=mesh['grp'=1,'comp'=2,'row'=4] {'row'}, use_global_device_ids=true, to_apply=%region_24.0 | all-reduce | flops 1024 | bytes 8192 | tf_op jit(solution)/shard_map/psum | solution.py:36
  143.6 26.9 %all-reduce.8.cloned.1.call-done = f32[2,512,128]{2,1,0:T(8,128)} async-done(((f32[2,512,128]{2,1,0:T(8,128)}), f32[2,512,128]{2,1,0:T(8,128)}) %all-reduce.8.cloned.1.call-update) | async-done | bytes 524304 | tf_op jit(solution)/shard_map/psum | solution.py:36
  170.5 2.0 %broadcast_divide_fusion = f32[2,512,128]{2,1,0:T(8,128)} fusion(f32[2,512,128]{2,1,0:T(8,128)} %all-reduce.8.cloned.1.call-done, f32[2,512]{1,0:T(2,128)S(1)} %get-tuple-element.4), kind=kLoop, calls=%fused_computation.30 | loop fusion | flops 131072 | bytes 1052672 | tf_op jit(solution)/shard_map/div | solution.py:37
  (20 shorter events, 9.1 us)
Async XLA Ops:
  7.2 2.7 %copy-start = (bf16[1024,256]{1,0:T(8,128)(2,1)S(1)}, bf16[1024,256]{1,0:T(8,128)(2,1)}, u32[]{:S(2)}) copy-start(bf16[1024,256]{1,0:T(8,128)(2,1)} %param.4) | copy-start | bytes 1572868
  7.2 55.0 %all-reduce.4.cloned.1.call-start = ((), (), s32[]{:S(2)}) async-start(), calls=%async_computation | async-start | bytes 1048576 | tf_op jit(solution)/shard_map/psum | solution.py:36
  32.8 79.9 %all-reduce.6.cloned.1.call-start = ((), (), s32[]{:S(2)}) async-start(), calls=%async_computation.1 | async-start | bytes 1048576 | tf_op jit(solution)/shard_map/psum | solution.py:36
  84.7 85.8 %all-reduce.8.cloned.1.call-start = ((), (), s32[]{:S(2)}) async-start(), calls=%async_computation.2 | async-start | bytes 1048576 | tf_op jit(solution)/shard_map/psum | solution.py:36
  131.5 3.4 %copy-start.1 = (f32[2,512,1024]{2,1,0:T(8,128)S(1)}, f32[2,512,1024]{2,1,0:T(8,128)}, u32[]{:S(2)}) copy-start(f32[2,512,1024]{2,1,0:T(8,128)} %get-tuple-element.17) | copy-start | bytes 12582916
Sparse Core Ops, SparseCore 0:
  32.9 29.2 all-reduce.3
  84.8 27.7 all-reduce.5
  142.5 27.9 all-reduce.7
where the time goes:
time: 180 us; the launch traced here: 179 us
  waiting for transfers between devices  66.4 us (37%)
  blocking collectives  48.9 us (27%)
  other arithmetic  25 us (14%)
  matrix products  23.2 us (13%)
  between operations  13.8 us (8%)
    psum x3, waiting for transfers between devices, local_fit(): counts, stat_sum = lax.psum((counts, stat_sum), 'row')  66.3 us
    psum x3, blocking collectives, local_fit(): counts, stat_sum = lax.psum((counts, stat_sum), 'row')  17.7 us
    pmax x3, blocking collectives, local_fit(): row_max = lax.pmax(jnp.max(logits, axis=2), 'comp')  16.2 us
    psum x3, blocking collectives, local_fit(): row_sum = lax.psum(jnp.sum(shifted, axis=2), 'comp')  15 us
    dot_general x3, matrix products, local_fit(): jnp.einsum('snh,skh->snk', x_fits, mean_vecs.astype(jnp.bfloat16), prefer...  14.1 us
    dot_general x3, matrix products, local_fit(): jnp.einsum('snk,snh->skh', resp_f.astype(jnp.bfloat16), x_fits, preferred...  9.11 us
    reduce_sum x3, other arithmetic, local_fit(): counts = jnp.sum(resp_f, axis=1)  9 us
    reduce_sum x3, other arithmetic, local_fit(): row_sum = lax.psum(jnp.sum(shifted, axis=2), 'comp')  8.27 us
  transfers between devices with their start and end apart: 3, of which 3 were waited for; matrix products, arithmetic and copies ran while one was open for 4% of the time, Pallas kernels for 0%

commit v1 on v0

v1 whole, which is shorter than its diff:
```python
import functools

import jax
import jax.numpy as jnp
from jax import lax
from jax.experimental import pallas as pl
from jax.experimental.pallas import tpu as pltpu
from jax.sharding import PartitionSpec as P

EPS_COUNT = 1e-6
PRIOR_ALPHA = 1e-3
LOG2E = 1.4426950408889634
LN2 = 0.6931471805599453
LANES = 128
TILE = 256

MESH = pl.DeviceIdType.MESH
F32 = jnp.float32
BF16 = jnp.bfloat16
NT = (((1,), (1,)), ((), ()))


def em_kernel(
    sweeps, total_pts, total_comp,
    temp_ref, xl_ref, mu_in, lp_in,
    mu_out, lp_out, lse_out,
    xg, mub, cc, ee, mm, stats, rr, ssum, nacc, lse2, lse_in, aux,
    s_own, r_own, s_x, r_x, s_rel, r_rel, s_st, r_st, s_lse, r_lse, s_fin, r_fin, s_frl, r_frl, s_aux, r_aux,
):
    row = lax.axis_index("row")
    y = lax.axis_index("comp")
    x = row // 2
    core = row % 2
    me = 2 * y + core
    mate = 2 * x + 1 - core
    across = 2 * (1 - x) + core
    across_mate = 2 * (1 - x) + 1 - core

    n_rows = xl_ref.shape[0]
    n_comp = mub.shape[0]
    blocks = xg.shape[0] // n_rows
    tiles = n_rows // TILE
    halves = TILE // LANES
    fit_col = pl.ds(pl.multiple_of(x * LANES, LANES), LANES)
    other_col = pl.ds(pl.multiple_of((1 - x) * LANES, LANES), LANES)
    my_comps = pl.ds(pl.multiple_of(core * n_comp, n_comp), n_comp)

    d_mate = {"row": mate}
    d_across = {"row": across}
    d_across_mate = {"row": across_mate}
    d_y = {"comp": 1 - y}
    d_y_mate = {"comp": 1 - y, "row": mate}

    def remote(src, dst, ssem, rsem, dev):
        return pltpu.make_async_remote_copy(src, dst, ssem, rsem, device_id=dev, device_id_type=MESH)

    barrier = pltpu.get_barrier_semaphore()
    for dev in (d_mate, d_across, d_across_mate, d_y, d_y_mate):
        pl.semaphore_signal(barrier, inc=1, device_id=dev, device_id_type=MESH)
    pl.semaphore_wait(barrier, 5)

    def rows_of(block, j):
        return pl.ds(pl.multiple_of(block * n_rows + j * TILE, TILE), TILE)

    own = remote(xl_ref.at[:, fit_col], xg.at[pl.ds(pl.multiple_of(row * n_rows, n_rows), n_rows), :],
                 s_own, r_own, d_mate)
    own.start()
    xs = []
    for j in range(tiles):
        c = remote(xl_ref.at[pl.ds(j * TILE, TILE), other_col], xg.at[rows_of(row, j), :], s_x.at[j], r_x.at[j], d_across)
        c.start()
        xs.append(c)

    xg[pl.ds(pl.multiple_of(row * n_rows, n_rows), n_rows), :] = xl_ref[:, fit_col]

    def set_means(sweep, mean, logw):
        mub[...] = mean.astype(BF16)
        sq = jnp.sum(mean * mean, axis=1, keepdims=True)
        cc[...] = jnp.broadcast_to(LOG2E * (logw - temp_ref[sweep] * sq), cc.shape)

    logw = jnp.transpose(jnp.broadcast_to(lp_in[pl.ds(x, 1), my_comps], (LANES, n_comp)))
    set_means(0, mu_in[x, my_comps, :], logw)

    def e_tile(sweep, block, j):
        t = block * tiles + j
        scale = (2.0 * LOG2E) * temp_ref[sweep]
        a = lax.dot_general(mub[...], xg[rows_of(block, j), :], NT, preferred_element_type=F32)
        for h in range(halves):
            z = a[:, h * LANES:(h + 1) * LANES] * scale + cc[...]
            m = jnp.max(z, axis=0, keepdims=True)
            e = jnp.exp2(z - m)
            r = jnp.sum(e, axis=0, keepdims=True)
            ee[t, :, h * LANES:(h + 1) * LANES] = e
            mm[t, h:h + 1, :] = m
            stats[sweep, me, t, h:h + 1, :] = m + jnp.log2(r)

    def st_copy(sweep, block, k):
        part = stats.at[sweep, me, pl.ds(block * tiles, tiles)]
        return remote(part, part, s_st.at[sweep, block, k], r_st.at[sweep, block, k],
                      (d_mate, d_y, d_y_mate)[k])

    def send_stats(sweep, block):
        for k in range(3):
            st_copy(sweep, block, k).start()

    def m_block(sweep, block, first):
        for k in range(3):
            st_copy(sweep, block, k).wait_recv()
        acc = None
        for j in range(tiles):
            t = block * tiles + j
            parts = [stats[sweep, d, t] for d in range(4)]
            top = jnp.maximum(jnp.maximum(parts[0], parts[1]), jnp.maximum(parts[2], parts[3]))
            tot = sum(jnp.exp2(p - top) for p in parts)
            lse = top + jnp.log2(tot)
            lse2[t] = lse
            w = jnp.exp2(mm[t] - lse)
            for h in range(halves):
                r = ee[t, :, h * LANES:(h + 1) * LANES] * w[h:h + 1, :]
                acc = r if acc is None else acc + r
                rr[:, j * TILE + h * LANES:j * TILE + (h + 1) * LANES] = r.astype(BF16)
        pts = xg[pl.ds(pl.multiple_of(block * n_rows, n_rows), n_rows), :]
        s = jnp.dot(rr[...], pts, preferred_element_type=F32)
        if first:
            ssum[...] = s
            nacc[...] = acc
        else:
            ssum[...] += s
            nacc[...] += acc

    def finish():
        n = jnp.sum(nacc[...], axis=1, keepdims=True)
        mean = ssum[...] / (n + EPS_COUNT)
        logw = jnp.log((n + PRIOR_ALPHA) / (total_pts + total_comp * PRIOR_ALPHA))
        return mean, logw

    for j in range(tiles):
        e_tile(0, row, j)
    send_stats(0, row)
    own.wait_recv()
    for j in range(tiles):
        e_tile(0, mate, j)
    send_stats(0, mate)
    relays = []
    for j in range(tiles):
        xs[j].wait_recv()
        part = xg.at[rows_of(across, j), :]
        c = remote(part, part, s_rel.at[j], r_rel.at[j], d_mate)
        c.start()
        relays.append(c)
        e_tile(0, across, j)
        if j:
            relays[j - 1].wait_recv()
            e_tile(0, across_mate, j - 1)
    send_stats(0, across)
    relays[-1].wait_recv()
    e_tile(0, across_mate, tiles - 1)
    send_stats(0, across_mate)
    for i, block in enumerate((row, mate, across, across_mate)):
        m_block(0, block, i == 0)

    for sweep in range(1, sweeps):
        mean, logw = finish()
        set_means(sweep, mean, logw)
        for block in range(blocks):
            for j in range(tiles):
                e_tile(sweep, block, j)
            send_stats(sweep, block)
        for block in range(blocks):
            m_block(sweep, block, block == 0)

    last = remote(lse2.at[pl.ds(across * tiles, tiles)], lse_in, s_lse, r_lse, d_across)
    last.start()
    mean, logw = finish()
    mu_out[x, my_comps, :] = mean
    parts = 2
    step = n_comp // parts
    fins = []
    for p in range(parts):
        piece = mu_out.at[x, pl.ds(pl.multiple_of(core * n_comp + p * step, step), step), :]
        c = remote(piece, piece, s_fin.at[0, p], r_fin.at[0, p], d_across)
        c.start()
        fins.append(c)
    piece = mu_out.at[x, my_comps, :]
    to_mate = remote(piece, piece, s_fin.at[1, 0], r_fin.at[1, 0], d_mate)
    to_mate.start()
    flat = jnp.transpose(jnp.broadcast_to(logw, (n_comp, LANES)))[0:1, :]
    for h in range(n_comp // LANES):
        aux[row, h:h + 1, :] = flat[:, h * LANES:(h + 1) * LANES]
    auxs = []
    for k, dev in enumerate((d_mate, d_across, d_across_mate)):
        c = remote(aux.at[row], aux.at[row], s_aux.at[k], r_aux.at[k], dev)
        c.start()
        auxs.append(c)

    ones = jnp.ones((8, LANES), BF16)
    last.wait_recv()
    for s in range(2):
        xf = xl_ref[:, s * LANES:(s + 1) * LANES].astype(F32)
        xx = xf * xf
        hi = xx.astype(BF16)
        lo = (xx - hi.astype(F32)).astype(BF16)
        sq = lax.dot_general(ones, hi, NT, preferred_element_type=F32)
        sq = sq + lax.dot_general(ones, lo, NT, preferred_element_type=F32)
        for j in range(tiles):
            val = jnp.where(x == s, lse2[row * tiles + j], lse_in[j])
            for h in range(halves):
                at = slice(j * TILE + h * LANES, j * TILE + (h + 1) * LANES)
                lse_out[s:s + 1, at] = val[h:h + 1, :] * LN2 - temp_ref[sweeps - 1] * sq[0:1, at]

    frels = []
    for p in range(parts):
        fins[p].wait_recv()
        piece = mu_out.at[1 - x, pl.ds(pl.multiple_of(core * n_comp + p * step, step), step), :]
        c = remote(piece, piece, s_frl.at[p], r_frl.at[p], d_mate)
        c.start()
        frels.append(c)
    for c in auxs:
        c.wait_recv()
    for b in range(blocks):
        for h in range(n_comp // LANES):
            at = (b % 2) * n_comp + h * LANES
            lp_out[b // 2:b // 2 + 1, at:at + LANES] = aux[b, h:h + 1, :]
    to_mate.wait_recv()
    for c in frels:
        c.wait_recv()

    for c in [own, to_mate, last] + xs + relays + fins + frels + auxs:
        c.wait_send()
    for sweep in range(sweeps):
        for block in range(blocks):
            for k in range(3):
                st_copy(sweep, block, k).wait_send()


def solution(mesh):
    rows_size = mesh.shape["row"]
    comp_size = mesh.shape["comp"]

    def local_fit(x_local, mu_init, logpi_init, inv_temp):
        n_rows = x_local.shape[0]
        half = x_local.shape[1] // 2
        n_half = mu_init.shape[1]
        n_comp = n_half // 2
        sweeps = inv_temp.shape[0]
        total_pts = n_rows * rows_size
        n_tiles = total_pts // TILE
        tiles = n_rows // TILE
        halves = TILE // LANES
        vmem = pl.BlockSpec(memory_space=pltpu.VMEM)
        dma = pltpu.SemaphoreType.DMA
        return pl.pallas_call(
            functools.partial(em_kernel, sweeps, total_pts, n_half * comp_size),
            out_shape=(
                jax.ShapeDtypeStruct(mu_init.shape, F32),
                jax.ShapeDtypeStruct(logpi_init.shape, F32),
                jax.ShapeDtypeStruct((2, n_rows), F32),
            ),
            in_specs=[pl.BlockSpec(memory_space=pltpu.SMEM), vmem, vmem, vmem],
            out_specs=(vmem, vmem, vmem),
            scratch_shapes=[
                pltpu.VMEM((total_pts, half), BF16),
                pltpu.VMEM((n_comp, half), BF16),
                pltpu.VMEM((n_comp, LANES), F32),
                pltpu.VMEM((n_tiles, n_comp, TILE), F32),
                pltpu.VMEM((n_tiles, halves, LANES), F32),
                pltpu.VMEM((sweeps, 4, n_tiles, halves, LANES), F32),
                pltpu.VMEM((n_comp, n_rows), BF16),
                pltpu.VMEM((n_comp, half), F32),
                pltpu.VMEM((n_comp, LANES), F32),
                pltpu.VMEM((n_tiles, halves, LANES), F32),
                pltpu.VMEM((tiles, halves, LANES), F32),
                pltpu.VMEM((rows_size, n_comp // LANES, LANES), F32),
                dma, dma, dma((tiles,)), dma((tiles,)), dma((tiles,)), dma((tiles,)),
                dma((sweeps, rows_size, 3)), dma((sweeps, rows_size, 3)),
                dma, dma, dma((2, 2)), dma((2, 2)), dma((2,)), dma((2,)), dma((3,)), dma((3,)),
            ],
            compiler_params=pltpu.CompilerParams(collective_id=0, has_side_effects=True),
        )(inv_temp, x_local, mu_init, logpi_init)

    return jax.shard_map(
        local_fit,
        mesh=mesh,
        in_specs=(P(("grp", "row"), None), P(None, ("grp", "comp"), None), P(None, ("grp", "comp")), P()),
        out_specs=(P(None, ("grp", "comp"), None), P(None, ("grp", "comp")), P(None, ("grp", "row"))),
        check_vma=False,
    )
```

time: 180 us -> 38.3 us (0.21)
  waiting for transfers between devices: 66.4 us -> 0 us
  blocking collectives: 48.9 us -> 0 us
  Pallas kernels: 0 us -> 34.3 us
  other arithmetic: 25 us -> 0 us
  matrix products: 23.2 us -> 0 us
  between operations: 13.8 us -> 0.65 us
    psum x3 -> x0, waiting for transfers between devices: 66.3 us -> none  [local_fit(): counts, stat_sum = lax.psum((counts, stat_sum), 'row')]
    pallas_call x0 -> x1, Pallas kernels: none -> 34.3 us  [local_fit(): pl.pallas_call(functools.partial(em_kernel, sweeps, total_pts, n_half * c...]
    psum x6 -> x0, blocking collectives: 32.7 us -> none  [the longest x3 17.7 us: local_fit(): counts, stat_sum = lax.psum((counts, stat_sum), 'row')]
    dot_general x6 -> x0, matrix products: 23.2 us -> none  [the longest x3 14.1 us: local_fit(): jnp.einsum('snh,skh->snk', x_fits, mean_vecs.astype(jnp.bfloat16), prefer...]
    reduce_sum x10 -> x0, other arithmetic: 21.7 us -> none  [the longest x3 9 us: local_fit(): counts = jnp.sum(resp_f, axis=1)]
    pmax x3 -> x0, blocking collectives: 16.2 us -> none  [local_fit(): row_max = lax.pmax(jnp.max(logits, axis=2), 'comp')]
    unnamed x4 -> x7, local copies, waits for them, and re-layouts: 0.36 us -> 3.17 us
    div x1 -> x0, other arithmetic: 2.04 us -> none  [local_fit(): mean_vecs = stat_sum / (counts[:, :, None] + EPS_COUNT)]
  transfers between devices with their start and end apart: 3 -> 0, of which waited for: 3 -> 0; matrix products, arithmetic and copies ran while one was open for 4% -> 0% of each run, Pallas kernels for 0% -> 0%
where the time goes in v1:
time: 38.3 us; the launch traced here: 38.1 us
  Pallas kernels  34.3 us (90%)
  local copies, waits for them, and re-layouts  3.17 us (8%)
  between operations  0.65 us (2%)
    pallas_call x1, Pallas kernels, local_fit(): pl.pallas_call(functools.partial(em_kernel, sweeps, total_pts, n_half * c...  34.3 us
    unnamed x7, local copies, waits for them, and re-layouts  3.17 us

profile of v1, /device:TPU:0, one launch (start us, length us, event | category | flops | bytes accessed | tf_op | source)
XLA Modules:
  0.0 38.1 jit_solution(14332473463340081955)
XLA Ops:
  0.6 34.3 %shard_map.67 = (f32[2,512,128]{2,1,0:T(8,128)}, f32[2,512]{1,0:T(2,128)}, f32[2,1024]{1,0:T(2,128)}) custom-call(f32[3]{0:T(128)} %temp_ref.1, bf16[1024,256]{1,0:T(8,128)(2,1)} %xl_ref.1, f32[2,512,128]{2,1,0:T(8,128)} %mu_in.1, f32[2,512]{1,0:T(2,128)} %lp_in.1), custom_call_target="tpu_custom_call" | custom-call | tf_op jit(solution)/shard_map/pallas_call | solution.py:252
  34.9 0.0 copy-start.1
  35.0 1.9 %copy.10 = f32[2,512,128]{2,1,0:T(8,128)} copy(f32[2,512,128]{2,1,0:T(8,128)} %get-tuple-element.6) | data formatting | bytes 1048576
  36.8 0.0 copy-done.1
  36.8 0.0 copy-start
  36.8 0.6 %copy.11 = f32[2,512]{1,0:T(2,128)} copy(f32[2,512]{1,0:T(2,128)S(1)} %copy-done.1) | data formatting | bytes 8192
  37.4 0.1 copy-done
  37.5 0.6 %copy.12 = f32[2,1024]{1,0:T(2,128)} copy(f32[2,1024]{1,0:T(2,128)S(1)} %copy-done) | data formatting | bytes 16384
Async XLA Ops:
  34.9 1.9 %copy-start.1 = (f32[2,512]{1,0:T(2,128)S(1)}, f32[2,512]{1,0:T(2,128)}, u32[]{:S(2)}) copy-start(f32[2,512]{1,0:T(2,128)} %get-tuple-element.7) | copy-start | bytes 12292
  36.8 0.7 %copy-start = (f32[2,1024]{1,0:T(2,128)S(1)}, f32[2,1024]{1,0:T(2,128)}, u32[]{:S(2)}) copy-start(f32[2,1024]{1,0:T(2,128)} %get-tuple-element.8) | copy-start | bytes 24580

commit v2 on v1

v2 whole, which is shorter than its diff:
```python
import functools

import jax
import jax.numpy as jnp
from jax import lax
from jax.experimental import pallas as pl
from jax.experimental.pallas import tpu as pltpu
from jax.sharding import PartitionSpec as P

EPS_COUNT = 1e-6
PRIOR_ALPHA = 1e-3
LOG2E = 1.4426950408889634
LN2 = 0.6931471805599453
LANES = 128
TILE = 256
PIECES = 4

MESH = pl.DeviceIdType.MESH
F32 = jnp.float32
BF16 = jnp.bfloat16
NT = (((1,), (1,)), ((), ()))


def em_kernel(
    sweeps, total_pts, total_comp,
    temp_in, x_in, mu_in, lp_in,
    mu_out, lp_out, lse_out,
    temp_ref, xo, xg, mu0, lp0, mub, cc, ee, mm, stats, rr, ssum, nacc, lse2, lse_in, aux,
    s_in, s_own, r_own, s_x, r_x, s_rel, r_rel, s_st, r_st, s_lse, r_lse,
    s_fin, r_fin, s_mate, r_mate, s_frl, r_frl, s_aux, r_aux,
):
    row = lax.axis_index("row")
    y = lax.axis_index("comp")
    x = row // 2
    core = row % 2
    me = 2 * y + core
    mate = 2 * x + 1 - core
    across = 2 * (1 - x) + core
    across_mate = 2 * (1 - x) + 1 - core

    n_rows = xo.shape[0]
    n_comp = mub.shape[0]
    blocks = xg.shape[0] // n_rows
    tiles = n_rows // TILE
    halves = TILE // LANES
    fit_col = pl.ds(pl.multiple_of(x * LANES, LANES), LANES)
    other_col = pl.ds(pl.multiple_of((1 - x) * LANES, LANES), LANES)
    my_comps = pl.ds(pl.multiple_of(core * n_comp, n_comp), n_comp)
    my_rows = pl.ds(pl.multiple_of(row * n_rows, n_rows), n_rows)

    d_mate = {"row": mate}
    d_across = {"row": across}
    d_across_mate = {"row": across_mate}
    d_y = {"comp": 1 - y}
    d_y_mate = {"comp": 1 - y, "row": mate}

    def drain(ref, sem):
        pltpu.make_async_copy(ref, ref, sem).wait()

    def remote(src, dst, ssem, rsem, dev):
        return pltpu.make_async_remote_copy(src, dst, ssem, rsem, device_id=dev, device_id_type=MESH)

    loads = [
        pltpu.make_async_copy(src, dst, s_in.at[i])
        for i, (src, dst) in enumerate((
            (x_in.at[:, other_col], xo),
            (x_in.at[:, fit_col], xg.at[my_rows, :]),
            (mu_in.at[x, my_comps, :], mu0),
            (lp_in, lp0),
            (temp_in, temp_ref),
        ))
    ]
    barrier = pltpu.get_barrier_semaphore()
    for dev in (d_mate, d_across, d_across_mate, d_y, d_y_mate):
        pl.semaphore_signal(barrier, inc=1, device_id=dev, device_id_type=MESH)
    for c in loads:
        c.start()
    with jax.named_scope("barrier"):
        pl.semaphore_wait(barrier, 5)
    with jax.named_scope("loads"):
        for c in loads:
            c.wait()

    def rows_of(block, j):
        return pl.ds(pl.multiple_of(block * n_rows + j * TILE, TILE), TILE)

    xs = []
    for j in range(tiles):
        c = remote(xo.at[pl.ds(j * TILE, TILE), :], xg.at[rows_of(row, j), :], s_x, r_x.at[j], d_across)
        c.start()
        xs.append(c)
    own = remote(xg.at[my_rows, :], xg.at[my_rows, :], s_own, r_own, d_mate)
    own.start()

    def set_means(sweep, mean, logw):
        mub[...] = mean.astype(BF16)
        sq = jnp.sum(mean * mean, axis=1, keepdims=True)
        cc[...] = jnp.broadcast_to(LOG2E * (logw - temp_ref[sweep] * sq), cc.shape)

    logw = jnp.transpose(jnp.broadcast_to(lp0[pl.ds(x, 1), my_comps], (LANES, n_comp)))
    set_means(0, mu0[...], logw)

    def cross(block, j):
        return lax.dot_general(mub[...], xg[rows_of(block, j), :], NT, preferred_element_type=F32)

    def e_tile(sweep, block, j, a):
        t = block * tiles + j
        scale = (2.0 * LOG2E) * temp_ref[sweep]
        for h in range(halves):
            z = a[:, h * LANES:(h + 1) * LANES] * scale + cc[...]
            m = jnp.max(z, axis=0, keepdims=True)
            e = jnp.exp2(z - m)
            r = jnp.sum(e, axis=0, keepdims=True)
            ee[t, :, h * LANES:(h + 1) * LANES] = e
            mm[t, h:h + 1, :] = m
            stats[sweep, me, t, h:h + 1, :] = m + jnp.log2(r)

    def st_copy(sweep, block, k):
        part = stats.at[sweep, me, pl.ds(block * tiles, tiles)]
        return remote(part, part, s_st, r_st.at[sweep, block], (d_mate, d_y, d_y_mate)[k])

    def send_stats(sweep, block):
        for k in (1, 2, 0):
            st_copy(sweep, block, k).start()

    def e_blocks(sweep, todo):
        order = [(block, j) for block in todo for j in range(tiles)]
        ahead = cross(*order[0])
        for i, (block, j) in enumerate(order):
            a = ahead
            if i + 1 < len(order):
                ahead = cross(*order[i + 1])
            e_tile(sweep, block, j, a)
            if j == tiles - 1:
                send_stats(sweep, block)

    def m_blocks(sweep, todo, first):
        with jax.named_scope("stwait"):
            for block in todo:
                drain(stats.at[sweep, pl.ds(0, 3), pl.ds(block * tiles, tiles)], r_st.at[sweep, block])
        with jax.named_scope("mblock"):
            m_blocks_(sweep, todo, first)

    def m_blocks_(sweep, todo, first):
        for i, block in enumerate(todo):
            ws = []
            for j in range(tiles):
                t = block * tiles + j
                parts = [stats[sweep, d, t] for d in range(4)]
                top = jnp.maximum(jnp.maximum(parts[0], parts[1]), jnp.maximum(parts[2], parts[3]))
                tot = (jnp.exp2(parts[0] - top) + jnp.exp2(parts[1] - top)) + (
                    jnp.exp2(parts[2] - top) + jnp.exp2(parts[3] - top))
                lse = top + jnp.log2(tot)
                lse2[t] = lse
                w = jnp.exp2(mm[t] - lse)
                ws += [w[h:h + 1, :] for h in range(halves)]
            for k in range(0, n_comp, 16):
                acc = None if first and i == 0 else nacc[k:k + 16, :]
                for v, w in enumerate(ws):
                    r = ee[block * tiles + v // halves, k:k + 16, (v % halves) * LANES:(v % halves + 1) * LANES] * w
                    acc = r if acc is None else acc + r
                    rr[block, k:k + 16, v * LANES:(v + 1) * LANES] = r.astype(BF16)
                nacc[k:k + 16, :] = acc
            pts = xg[pl.ds(pl.multiple_of(block * n_rows, n_rows), n_rows), :]
            s = jnp.dot(rr[block], pts, preferred_element_type=F32)
            if first and i == 0:
                ssum[...] = s
            else:
                ssum[...] += s

    def finish():
        n = jnp.sum(nacc[...], axis=1, keepdims=True)
        mean = ssum[...] / (n + EPS_COUNT)
        logw = jnp.log((n + PRIOR_ALPHA) / (total_pts + total_comp * PRIOR_ALPHA))
        return mean, logw

    with jax.named_scope("e_own"):
        e_blocks(0, (row,))
    with jax.named_scope("w_own"):
        own.wait_recv()
    with jax.named_scope("e_mate"):
        e_blocks(0, (mate,))
    relays = []
    for j in range(tiles):
        with jax.named_scope(f"w_x{j}"):
            xs[j].wait_recv()
        part = xg.at[rows_of(across, j), :]
        c = remote(part, part, s_rel, r_rel.at[j], d_mate)
        c.start()
        relays.append(c)
        e_tile(0, across, j, cross(across, j))
        if j == tiles - 1:
            send_stats(0, across)
        if j:
            with jax.named_scope(f"w_rel{j}"):
                relays[j - 1].wait_recv()
            e_tile(0, across_mate, j - 1, cross(across_mate, j - 1))
        if j == 2:
            m_blocks(0, (row, mate), True)
    with jax.named_scope("w_rel4"):
        relays[-1].wait_recv()
    e_tile(0, across_mate, tiles - 1, cross(across_mate, tiles - 1))
    send_stats(0, across_mate)
    m_blocks(0, (across,), False)
    m_blocks(0, (across_mate,), False)

    for sweep in range(1, sweeps):
        with jax.named_scope("finish"):
            mean, logw = finish()
            set_means(sweep, mean, logw)
        with jax.named_scope("esweep"):
            e_blocks(sweep, range(blocks))
        for block in range(blocks):
            m_blocks(sweep, (block,), block == 0)

    mean, logw = finish()
    mu_out[x, my_comps, :] = mean
    step = n_comp // PIECES
    fins = []

    def piece(fit, p):
        return mu_out.at[fit, pl.ds(pl.multiple_of(core * n_comp + p * step, step), step), :]

    for p in range(PIECES):
        c = remote(piece(x, p), piece(x, p), s_fin, r_fin.at[p], d_across)
        c.start()
        fins.append(c)
    part = mu_out.at[x, my_comps, :]
    to_mate = remote(part, part, s_mate, r_mate, d_mate)
    to_mate.start()
    last = remote(lse2.at[pl.ds(across * tiles, tiles)], lse_in, s_lse, r_lse, d_across)
    last.start()
    flat = jnp.transpose(jnp.broadcast_to(logw, (n_comp, LANES)))[0:1, :]
    for h in range(n_comp // LANES):
        aux[row, h:h + 1, :] = flat[:, h * LANES:(h + 1) * LANES]
    auxs = []
    for k, dev in enumerate((d_mate, d_across, d_across_mate)):
        c = remote(aux.at[row], aux.at[row], s_aux, r_aux, dev)
        c.start()
        auxs.append(c)

    ones = jnp.ones((8, LANES), BF16)

    def sq_rows(pts):
        xf = pts.astype(F32)
        xx = xf * xf
        hi = xx.astype(BF16)
        lo = (xx - hi.astype(F32)).astype(BF16)
        sq = lax.dot_general(ones, hi, NT, preferred_element_type=F32)
        return sq + lax.dot_general(ones, lo, NT, preferred_element_type=F32)

    def write_lse(sq_own, sq_other):
        for s in range(2):
            sq = jnp.where(x == s, sq_own, sq_other)
            for j in range(tiles):
                val = jnp.where(x == s, lse2[row * tiles + j], lse_in[j])
                for h in range(halves):
                    at = slice(j * TILE + h * LANES, j * TILE + (h + 1) * LANES)
                    lse_out[s:s + 1, at] = val[h:h + 1, :] * LN2 - temp_ref[sweeps - 1] * sq[0:1, at]

    with jax.named_scope("lse"):
        sq_own = sq_rows(xg[my_rows, :])
        sq_other = sq_rows(xo[...])
    frels = []
    for p in range(PIECES):
        with jax.named_scope(f"w_fin{p}"):
            fins[p].wait_recv()
        c = remote(piece(1 - x, p), piece(1 - x, p), s_frl, r_frl, d_mate)
        c.start()
        frels.append(c)
    with jax.named_scope("w_last"):
        last.wait_recv()
    write_lse(sq_own, sq_other)
    drain(aux.at[pl.ds(0, 3)], r_aux)
    for b in range(blocks):
        for h in range(n_comp // LANES):
            at = (b % 2) * n_comp + h * LANES
            lp_out[b // 2:b // 2 + 1, at:at + LANES] = aux[b, h:h + 1, :]
    with jax.named_scope("w_frel"):
        to_mate.wait_recv()
        drain(ssum, r_frl)
    with jax.named_scope("w_sends"):
        for c in (own, to_mate, last):
            c.wait_send()
        drain(xo, s_x)
        drain(xo, s_rel)
        drain(ssum, s_fin)
        drain(ssum, s_frl)
        drain(aux.at[pl.ds(0, 3)], s_aux)
        drain(stats.at[:, pl.ds(0, 3)], s_st)


def store_kernel(a, b, c, a_out, b_out, c_out, sem):
    copies = [
        pltpu.make_async_copy(src, dst, sem.at[i])
        for i, (src, dst) in enumerate(((a, a_out), (b, b_out), (c, c_out)))
    ]
    for c in copies:
        c.start()
    for c in copies:
        c.wait()


def solution(mesh):
    rows_size = mesh.shape["row"]
    comp_size = mesh.shape["comp"]

    def local_fit(x_local, mu_init, logpi_init, inv_temp):
        n_rows = x_local.shape[0]
        half = x_local.shape[1] // 2
        n_half = mu_init.shape[1]
        n_comp = n_half // 2
        sweeps = inv_temp.shape[0]
        total_pts = n_rows * rows_size
        n_tiles = total_pts // TILE
        tiles = n_rows // TILE
        halves = TILE // LANES
        vmem = pl.BlockSpec(memory_space=pltpu.VMEM)
        hbm = pl.BlockSpec(memory_space=pl.ANY)
        dma = pltpu.SemaphoreType.DMA
        outs = pl.pallas_call(
            functools.partial(em_kernel, sweeps, total_pts, n_half * comp_size),
            out_shape=(
                pltpu.VMEM(mu_init.shape, F32),
                pltpu.VMEM(logpi_init.shape, F32),
                pltpu.VMEM((2, n_rows), F32),
            ),
            in_specs=[hbm] * 4,
            out_specs=(vmem, vmem, vmem),
            scratch_shapes=[
                pltpu.SMEM((sweeps,), F32),
                pltpu.VMEM((n_rows, half), BF16),
                pltpu.VMEM((total_pts, half), BF16),
                pltpu.VMEM((n_comp, half), F32),
                pltpu.VMEM(logpi_init.shape, F32),
                pltpu.VMEM((n_comp, half), BF16),
                pltpu.VMEM((n_comp, LANES), F32),
                pltpu.VMEM((n_tiles, n_comp, TILE), F32),
                pltpu.VMEM((n_tiles, halves, LANES), F32),
                pltpu.VMEM((sweeps, 4, n_tiles, halves, LANES), F32),
                pltpu.VMEM((rows_size, n_comp, n_rows), BF16),
                pltpu.VMEM((n_comp, half), F32),
                pltpu.VMEM((n_comp, LANES), F32),
                pltpu.VMEM((n_tiles, halves, LANES), F32),
                pltpu.VMEM((tiles, halves, LANES), F32),
                pltpu.VMEM((rows_size, n_comp // LANES, LANES), F32),
                dma((5,)), dma, dma, dma, dma((tiles,)), dma, dma((tiles,)), dma, dma((sweeps, rows_size)), dma, dma,
                dma, dma((PIECES,)), dma, dma, dma, dma, dma, dma,
            ],
            compiler_params=pltpu.CompilerParams(collective_id=0, has_side_effects=True),
        )(inv_temp, x_local, mu_init, logpi_init)
        outs = [pltpu.with_memory_space_constraint(o, pltpu.VMEM) for o in outs]
        return pl.pallas_call(
            store_kernel,
            out_shape=tuple(jax.ShapeDtypeStruct(o.shape, F32) for o in outs),
            in_specs=[vmem] * 3,
            out_specs=(hbm, hbm, hbm),
            scratch_shapes=[dma((3,))],
        )(*outs)

    return jax.shard_map(
        local_fit,
        mesh=mesh,
        in_specs=(P(("grp", "row"), None), P(None, ("grp", "comp"), None), P(None, ("grp", "comp")), P()),
        out_specs=(P(None, ("grp", "comp"), None), P(None, ("grp", "comp")), P(None, ("grp", "row"))),
        check_vma=False,
    )
```

time: 38.3 us -> 33.4 us (0.87)
  local copies, waits for them, and re-layouts: 3.17 us -> 0 us
  Pallas kernels: 34.3 us -> 32.7 us
    unnamed x7 -> x0, local copies, waits for them, and re-layouts: 3.17 us -> none
    pallas_call x1, Pallas kernels: 34.3 us -> 31.9 us  [local_fit(): pl.pallas_call(functools.partial(em_kernel, sweeps, total_pts, n_half * c...]
    pallas_call x0 -> x1, Pallas kernels: none -> 0.83 us  [local_fit(): pl.pallas_call(store_kernel, out_shape=tuple((jax.ShapeDtypeStruct(o.shap...]
where the time goes in v2:
time: 33.4 us; the launch traced here: 33.3 us
  Pallas kernels  32.7 us (98%)
  between operations  0.64 us (2%)
    pallas_call x1, Pallas kernels, local_fit(): pl.pallas_call(functools.partial(em_kernel, sweeps, total_pts, n_half * c...  31.9 us
    pallas_call x1, Pallas kernels, local_fit(): pl.pallas_call(store_kernel, out_shape=tuple((jax.ShapeDtypeStruct(o.shap...  0.83 us

profile of v2, /device:TPU:0, one launch (start us, length us, event | category | flops | bytes accessed | tf_op | source)
XLA Modules:
  0.0 33.3 jit_solution(13492238487162167813)
XLA Ops:
  0.6 31.9 %shard_map.67 = (f32[2,512,128]{2,1,0:T(8,128)S(1)}, f32[2,512]{1,0:T(2,128)S(1)}, f32[2,1024]{1,0:T(2,128)S(1)}) custom-call(f32[3]{0:T(128)} %temp_in.1, bf16[1024,256]{1,0:T(8,128)(2,1)} %x_in.1, f32[2,512,128]{2,1,0:T(8,128)} %mu_in.1, f32[2,512]{1,0:T(2,128)} %lp_in.1), custom_call_target="tpu_custom_call" | custom-call | tf_op jit(solution)/shard_map/pallas_call | solution.py:321
  32.5 0.8 %shard_map.68 = (f32[2,512,128]{2,1,0:T(8,128)}, f32[2,512]{1,0:T(2,128)}, f32[2,1024]{1,0:T(2,128)}) custom-call(f32[2,512,128]{2,1,0:T(8,128)S(1)} %get-tuple-element.6.a, f32[2,512]{1,0:T(2,128)S(1)} %get-tuple-element.7.b, f32[2,1024]{1,0:T(2,128)S(1)} %get-tuple-element.8.c), custom_call_target="tpu_custom_call" | custom-call | tf_op jit(solution)/shard_map/pallas_call | solution.py:353

commit v3 on v2

--- a/solution.py
+++ b/solution.py
@@ -25,9 +25,10 @@
     sweeps, total_pts, total_comp,
     temp_in, x_in, mu_in, lp_in,
     mu_out, lp_out, lse_out,
-    temp_ref, xo, xg, mu0, lp0, mub, cc, ee, mm, stats, rr, ssum, nacc, lse2, lse_in, aux,
-    s_in, s_own, r_own, s_x, r_x, s_rel, r_rel, s_st, r_st, s_lse, r_lse,
-    s_fin, r_fin, s_mate, r_mate, s_frl, r_frl, s_aux, r_aux,
+    temp_ref, xo, xg, mu0, lp0, mub0, cc0, stats0, part, inbox, xsend, xin, nsend, nin,
+    mub, cc, ee, mm, stats, rr, ssum, nacc, lse2, lse_in, aux,
+    s_in, s_own, r_own, s_x, r_x, s_rel, r_rel, s_st0, r_st0, s_part, r_part, s_xs, r_xs, s_n, r_n,
+    s_st, r_st, s_lse, r_lse, s_fin, r_fin, s_mate, r_mate, s_frl, r_frl, s_aux, r_aux,
 ):
     row = lax.axis_index("row")
     y = lax.axis_index("comp")
@@ -46,6 +47,7 @@
     fit_col = pl.ds(pl.multiple_of(x * LANES, LANES), LANES)
     other_col = pl.ds(pl.multiple_of((1 - x) * LANES, LANES), LANES)
     my_comps = pl.ds(pl.multiple_of(core * n_comp, n_comp), n_comp)
+    mates_comps = pl.ds(pl.multiple_of((1 - core) * n_comp, n_comp), n_comp)
     my_rows = pl.ds(pl.multiple_of(row * n_rows, n_rows), n_rows)
 
     d_mate = {"row": mate}
@@ -65,7 +67,7 @@
         for i, (src, dst) in enumerate((
             (x_in.at[:, other_col], xo),
             (x_in.at[:, fit_col], xg.at[my_rows, :]),
-            (mu_in.at[x, my_comps, :], mu0),
+            (mu_in, mu0),
             (lp_in, lp0),
             (temp_in, temp_ref),
         ))
@@ -84,40 +86,147 @@
     def rows_of(block, j):
         return pl.ds(pl.multiple_of(block * n_rows + j * TILE, TILE), TILE)
 
-    xs = []
-    for j in range(tiles):
-        c = remote(xo.at[pl.ds(j * TILE, TILE), :], xg.at[rows_of(row, j), :], s_x, r_x.at[j], d_across)
-        c.start()
-        xs.append(c)
+    xs = [
+        remote(xo.at[pl.ds(j * TILE, TILE), :], xg.at[rows_of(row, j), :], s_x, r_x.at[j], d_across)
+        for j in range(tiles)
+    ]
+    relays = [
+        remote(xg.at[rows_of(across, j), :], xg.at[rows_of(across, j), :], s_rel, r_rel.at[j], d_mate)
+        for j in range(tiles)
+    ]
     own = remote(xg.at[my_rows, :], xg.at[my_rows, :], s_own, r_own, d_mate)
+    for c in xs[:-1]:
+        c.start()
     own.start()
 
-    def set_means(sweep, mean, logw):
-        mub[...] = mean.astype(BF16)
+    def means_to(sweep, mean, logw, mub_at, cc_at):
+        mub_at[...] = mean.astype(BF16)
         sq = jnp.sum(mean * mean, axis=1, keepdims=True)
-        cc[...] = jnp.broadcast_to(LOG2E * (logw - temp_ref[sweep] * sq), cc.shape)
-
-    logw = jnp.transpose(jnp.broadcast_to(lp0[pl.ds(x, 1), my_comps], (LANES, n_comp)))
-    set_means(0, mu0[...], logw)
-
-    def cross(block, j):
-        return lax.dot_general(mub[...], xg[rows_of(block, j), :], NT, preferred_element_type=F32)
-
-    def e_tile(sweep, block, j, a):
-        t = block * tiles + j
+        cc_at[...] = jnp.broadcast_to(LOG2E * (logw - temp_ref[sweep] * sq), cc_at.shape)
+
+    def column(flat):
+        return jnp.transpose(jnp.broadcast_to(flat, (LANES, n_comp)))
+
+    def e_tile(sweep, t, a, cc_at, stat):
         scale = (2.0 * LOG2E) * temp_ref[sweep]
         for h in range(halves):
-            z = a[:, h * LANES:(h + 1) * LANES] * scale + cc[...]
+            z = a[:, h * LANES:(h + 1) * LANES] * scale + cc_at[...]
             m = jnp.max(z, axis=0, keepdims=True)
             e = jnp.exp2(z - m)
             r = jnp.sum(e, axis=0, keepdims=True)
             ee[t, :, h * LANES:(h + 1) * LANES] = e
             mm[t, h:h + 1, :] = m
-            stats[sweep, me, t, h:h + 1, :] = m + jnp.log2(r)
+            stat[h:h + 1, :] = m + jnp.log2(r)
+
+    def lse_of(parts):
+        top = jnp.maximum(jnp.maximum(parts[0], parts[1]), jnp.maximum(parts[2], parts[3]))
+        tot = (jnp.exp2(parts[0] - top) + jnp.exp2(parts[1] - top)) + (
+            jnp.exp2(parts[2] - top) + jnp.exp2(parts[3] - top))
+        return top + jnp.log2(tot)
+
+    def m_region(lses, base, pts, slot, n_at, s_at, first):
+        ws = []
+        for j in range(tiles):
+            w = jnp.exp2(mm[base + j] - lses[j])
+            ws += [w[h:h + 1, :] for h in range(halves)]
+        for k in range(0, n_comp, 16):
+            acc = None if first else n_at[k:k + 16, :]
+            for v, w in enumerate(ws):
+                r = ee[base + v // halves, k:k + 16, (v % halves) * LANES:(v % halves + 1) * LANES] * w
+                acc = r if acc is None else acc + r
+                rr[slot, k:k + 16, v * LANES:(v + 1) * LANES] = r.astype(BF16)
+            n_at[k:k + 16, :] = acc
+        s = jnp.dot(rr[slot], pts, preferred_element_type=F32)
+        if first:
+            s_at[...] = s
+        else:
+            s_at[...] += s
+
+    def cross0(slot, j):
+        pts = xg[rows_of(row, j), :] if slot // 2 else xo[pl.ds(j * TILE, TILE), :]
+        return lax.dot_general(mub0[slot], pts, NT, preferred_element_type=F32)
+
+    def st0_copy(fo):
+        at = stats0.at[fo, pl.ds(2 * y, 2)]
+        return remote(at, at, s_st0, r_st0.at[fo], d_y)
+
+    for fo, fit in enumerate((1 - x, x)):
+        with jax.named_scope(f"set0_{fo}"):
+            for qo, comps in enumerate((mates_comps, my_comps)):
+                slot = 2 * fo + qo
+                means_to(0, mu0[fit, comps, :], column(lp0[pl.ds(fit, 1), comps]), mub0.at[slot], cc0.at[slot])
+        with jax.named_scope(f"e0_{fo}"):
+            order = [(2 * fo + qo, j) for qo in range(2) for j in range(tiles)]
+            ahead = cross0(*order[0])
+            for i, (slot, j) in enumerate(order):
+                a = ahead
+                if i + 1 < len(order):
+                    ahead = cross0(*order[i + 1])
+                e_tile(0, slot * tiles + j, a, cc0.at[slot], stats0.at[fo, 2 * y + slot % 2, j])
+        st0_copy(fo).start()
+
+    def part_copy(fo, k):
+        return remote(part.at[2 * fo, k], inbox.at[fo, k], s_part, r_part.at[fo, k], d_mate)
+
+    def m0(fo, qo):
+        slot = 2 * fo + qo
+        lses = [lse_of([stats0[fo, d, j] for d in range(4)]) for j in range(tiles)]
+        pts = xg[my_rows, :] if fo else xo[...]
+        m_region(lses, slot * tiles, pts, slot, part.at[slot, 1], part.at[slot, 0], True)
+
+    step = n_comp // PIECES
+    with jax.named_scope("w_st0_0"):
+        st0_copy(0).wait_recv()
+    with jax.named_scope("m0_0"):
+        m0(0, 0)
+    for k in range(2):
+        part_copy(0, k).start()
+    with jax.named_scope("m0_1"):
+        m0(0, 1)
+    with jax.named_scope("w_part0"):
+        part_copy(0, 0).wait_recv()
+    sums = []
+    for p in range(PIECES):
+        at = pl.ds(p * step, step)
+        xsend[at, :] = part[1, 0, at, :] + inbox[0, 0, at, :]
+        c = remote(xsend.at[at, :], xin.at[at, :], s_xs, r_xs, d_across)
+        c.start()
+        sums.append(c)
+    part_copy(0, 1).wait_recv()
+    flat = jnp.sum(jnp.transpose(part[1, 1] + inbox[0, 1]), axis=0, keepdims=True)
+    for h in range(n_comp // LANES):
+        nsend[h:h + 1, :] = flat[:, h * LANES:(h + 1) * LANES]
+    counts = remote(nsend, nin, s_n, r_n, d_across)
+    counts.start()
+    xs[-1].start()
+    with jax.named_scope("w_st0_1"):
+        st0_copy(1).wait_recv()
+    with jax.named_scope("m0_2"):
+        m0(1, 0)
+    for k in range(2):
+        part_copy(1, k).start()
+    with jax.named_scope("m0_3"):
+        m0(1, 1)
+    for j in range(tiles - 1):
+        with jax.named_scope(f"w_x{j}"):
+            xs[j].wait_recv()
+        relays[j].start()
+    with jax.named_scope("w_part1"):
+        for k in range(2):
+            part_copy(1, k).wait_recv()
+    with jax.named_scope("w_xin"):
+        counts.wait_recv()
+        drain(xsend, r_xs)
+    n_across = column(jnp.concatenate([nin[h:h + 1, :] for h in range(n_comp // LANES)], axis=1))
+    ssum[...] = part[3, 0] + inbox[1, 0] + xin[...]
+    n_first = jnp.sum(part[3, 1] + inbox[1, 1], axis=1, keepdims=True) + n_across
+
+    def cross(block, j):
+        return lax.dot_general(mub[...], xg[rows_of(block, j), :], NT, preferred_element_type=F32)
 
     def st_copy(sweep, block, k):
-        part = stats.at[sweep, me, pl.ds(block * tiles, tiles)]
-        return remote(part, part, s_st, r_st.at[sweep, block], (d_mate, d_y, d_y_mate)[k])
+        part = stats.at[sweep - 1, me, pl.ds(block * tiles, tiles)]
+        return remote(part, part, s_st, r_st.at[sweep - 1, block], (d_mate, d_y, d_y_mate)[k])
 
     def send_stats(sweep, block):
         for k in (1, 2, 0):
@@ -130,92 +239,62 @@
             a = ahead
             if i + 1 < len(order):
                 ahead = cross(*order[i + 1])
-            e_tile(sweep, block, j, a)
+            t = block * tiles + j
+            e_tile(sweep, t, a, cc, stats.at[sweep - 1, me, t])
             if j == tiles - 1:
                 send_stats(sweep, block)
 
-    def m_blocks(sweep, todo, first):
+    def m_block(sweep, block, first):
         with jax.named_scope("stwait"):
-            for block in todo:
-                drain(stats.at[sweep, pl.ds(0, 3), pl.ds(block * tiles, tiles)], r_st.at[sweep, block])
+            drain(stats.at[sweep - 1, pl.ds(0, 3), pl.ds(block * tiles, tiles)], r_st.at[sweep - 1, block])
         with jax.named_scope("mblock"):
-            m_blocks_(sweep, todo, first)
-
-    def m_blocks_(sweep, todo, first):
-        for i, block in enumerate(todo):
-            ws = []
+            lses = []
             for j in range(tiles):
                 t = block * tiles + j
-                parts = [stats[sweep, d, t] for d in range(4)]
-                top = jnp.maximum(jnp.maximum(parts[0], parts[1]), jnp.maximum(parts[2], parts[3]))
-                tot = (jnp.exp2(parts[0] - top) + jnp.exp2(parts[1] - top)) + (
-                    jnp.exp2(parts[2] - top) + jnp.exp2(parts[3] - top))
-                lse = top + jnp.log2(tot)
-                lse2[t] = lse
-                w = jnp.exp2(mm[t] - lse)
-                ws += [w[h:h + 1, :] for h in range(halves)]
-            for k in range(0, n_comp, 16):
-                acc = None if first and i == 0 else nacc[k:k + 16, :]
-                for v, w in enumerate(ws):
-                    r = ee[block * tiles + v // halves, k:k + 16, (v % halves) * LANES:(v % halves + 1) * LANES] * w
-                    acc = r if acc is None else acc + r
-                    rr[block, k:k + 16, v * LANES:(v + 1) * LANES] = r.astype(BF16)
-                nacc[k:k + 16, :] = acc
+                lses.append(lse_of([stats[sweep - 1, d, t] for d in range(4)]))
+                lse2[t] = lses[-1]
             pts = xg[pl.ds(pl.multiple_of(block * n_rows, n_rows), n_rows), :]
-            s = jnp.dot(rr[block], pts, preferred_element_type=F32)
-            if first and i == 0:
-                ssum[...] = s
-            else:
-                ssum[...] += s
-
-    def finish():
-        n = jnp.sum(nacc[...], axis=1, keepdims=True)
+            m_region(lses, block * tiles, pts, block, nacc, ssum, first)
+
+    def finish(n):
         mean = ssum[...] / (n + EPS_COUNT)
         logw = jnp.log((n + PRIOR_ALPHA) / (total_pts + total_comp * PRIOR_ALPHA))
         return mean, logw
 
-    with jax.named_scope("e_own"):
-        e_blocks(0, (row,))
-    with jax.named_scope("w_own"):
-        own.wait_recv()
-    with jax.named_scope("e_mate"):
-        e_blocks(0, (mate,))
-    relays = []
-    for j in range(tiles):
-        with jax.named_scope(f"w_x{j}"):
-            xs[j].wait_recv()
-        part = xg.at[rows_of(across, j), :]
-        c = remote(part, part, s_rel, r_rel.at[j], d_mate)
-        c.start()
-        relays.append(c)
-        e_tile(0, across, j, cross(across, j))
-        if j == tiles - 1:
-            send_stats(0, across)
-        if j:
-            with jax.named_scope(f"w_rel{j}"):
-                relays[j - 1].wait_recv()
-            e_tile(0, across_mate, j - 1, cross(across_mate, j - 1))
-        if j == 2:
-            m_blocks(0, (row, mate), True)
-    with jax.named_scope("w_rel4"):
-        relays[-1].wait_recv()
-    e_tile(0, across_mate, tiles - 1, cross(across_mate, tiles - 1))
-    send_stats(0, across_mate)
-    m_blocks(0, (across,), False)
-    m_blocks(0, (across_mate,), False)
-
+    with jax.named_scope("finish"):
+        mean, logw = finish(n_first)
+        means_to(1, mean, logw, mub, cc)
     for sweep in range(1, sweeps):
+        if sweep == 1:
+            with jax.named_scope("e_row"):
+                e_blocks(1, (row,))
+            with jax.named_scope("w_own"):
+                own.wait_recv()
+            with jax.named_scope("e_mate"):
+                e_blocks(1, (mate,))
+            with jax.named_scope("w_x3"):
+                xs[-1].wait_recv()
+            relays[-1].start()
+            with jax.named_scope("e_across"):
+                e_blocks(1, (across,))
+            with jax.named_scope("w_rel"):
+                for c in relays:
+                    c.wait_recv()
+            with jax.named_scope("e_across_mate"):
+                e_blocks(1, (across_mate,))
+            order = (row, mate, across, across_mate)
+        else:
+            with jax.named_scope("esweep"):
+                e_blocks(sweep, range(blocks))
+            order = range(blocks)
+        for i, block in enumerate(order):
+            m_block(sweep, block, i == 0)
         with jax.named_scope("finish"):
-            mean, logw = finish()
-            set_means(sweep, mean, logw)
-        with jax.named_scope("esweep"):
-            e_blocks(sweep, range(blocks))
-        for block in range(blocks):
-            m_blocks(sweep, (block,), block == 0)
-
-    mean, logw = finish()
+            mean, logw = finish(jnp.sum(nacc[...], axis=1, keepdims=True))
+            if sweep + 1 < sweeps:
+                means_to(sweep + 1, mean, logw, mub, cc)
+
     mu_out[x, my_comps, :] = mean
-    step = n_comp // PIECES
     fins = []
 
     def piece(fit, p):
@@ -225,8 +304,8 @@
         c = remote(piece(x, p), piece(x, p), s_fin, r_fin.at[p], d_across)
         c.start()
         fins.append(c)
-    part = mu_out.at[x, my_comps, :]
-    to_mate = remote(part, part, s_mate, r_mate, d_mate)
+    whole = mu_out.at[x, my_comps, :]
+    to_mate = remote(whole, whole, s_mate, r_mate, d_mate)
     to_mate.start()
     last = remote(lse2.at[pl.ds(across * tiles, tiles)], lse_in, s_lse, r_lse, d_across)
     last.start()
@@ -280,8 +359,11 @@
         to_mate.wait_recv()
         drain(ssum, r_frl)
     with jax.named_scope("w_sends"):
-        for c in (own, to_mate, last):
+        for c in (own, to_mate, last, counts):
             c.wait_send()
+        drain(stats0.at[:, pl.ds(0, 2)], s_st0)
+        drain(part.at[pl.ds(0, 2)], s_part)
+        drain(xsend, s_xs)
         drain(xo, s_x)
         drain(xo, s_rel)
         drain(ssum, s_fin)
@@ -331,20 +413,30 @@
                 pltpu.SMEM((sweeps,), F32),
                 pltpu.VMEM((n_rows, half), BF16),
                 pltpu.VMEM((total_pts, half), BF16),
+                pltpu.VMEM(mu_init.shape, F32),
+                pltpu.VMEM(logpi_init.shape, F32),
+                pltpu.VMEM((4, n_comp, half), BF16),
+                pltpu.VMEM((4, n_comp, LANES), F32),
+                pltpu.VMEM((2, 4, tiles, halves, LANES), F32),
+                pltpu.VMEM((4, 2, n_comp, LANES), F32),
+                pltpu.VMEM((2, 2, n_comp, LANES), F32),
                 pltpu.VMEM((n_comp, half), F32),
-                pltpu.VMEM(logpi_init.shape, F32),
+                pltpu.VMEM((n_comp, half), F32),
+                pltpu.VMEM((n_comp // LANES, LANES), F32),
+                pltpu.VMEM((n_comp // LANES, LANES), F32),
                 pltpu.VMEM((n_comp, half), BF16),
                 pltpu.VMEM((n_comp, LANES), F32),
                 pltpu.VMEM((n_tiles, n_comp, TILE), F32),
                 pltpu.VMEM((n_tiles, halves, LANES), F32),
-                pltpu.VMEM((sweeps, 4, n_tiles, halves, LANES), F32),
+                pltpu.VMEM((sweeps - 1, 4, n_tiles, halves, LANES), F32),
                 pltpu.VMEM((rows_size, n_comp, n_rows), BF16),
                 pltpu.VMEM((n_comp, half), F32),
                 pltpu.VMEM((n_comp, LANES), F32),
                 pltpu.VMEM((n_tiles, halves, LANES), F32),
                 pltpu.VMEM((tiles, halves, LANES), F32),
                 pltpu.VMEM((rows_size, n_comp // LANES, LANES), F32),
-                dma((5,)), dma, dma, dma, dma((tiles,)), dma, dma((tiles,)), dma, dma((sweeps, rows_size)), dma, dma,
+                dma((5,)), dma, dma, dma, dma((tiles,)), dma, dma((tiles,)), dma, dma((2,)), dma, dma((2, 2)),
+                dma, dma, dma, dma, dma, dma((sweeps - 1, rows_size)), dma, dma,
                 dma, dma((PIECES,)), dma, dma, dma, dma, dma, dma,
             ],
             compiler_params=pltpu.CompilerParams(collective_id=0, has_side_effects=True),

time: 33.4 us -> 31.6 us (0.946)
  Pallas kernels: 32.7 us -> 30.9 us
    pallas_call x1, Pallas kernels: 31.9 us -> 30.1 us  [local_fit(): pl.pallas_call(functools.partial(em_kernel, sweeps, total_pts, n_half * c...]
where the time goes in v3:
time: 31.6 us; the launch traced here: 31.5 us
  Pallas kernels  30.9 us (98%)
  between operations  0.64 us (2%)
    pallas_call x1, Pallas kernels, local_fit(): pl.pallas_call(functools.partial(em_kernel, sweeps, total_pts, n_half * c...  30.1 us
    pallas_call x1, Pallas kernels, local_fit(): pl.pallas_call(store_kernel, out_shape=tuple((jax.ShapeDtypeStruct(o.shap...  0.83 us

profile of v3, /device:TPU:0, one launch (start us, length us, event | category | flops | bytes accessed | tf_op | source)
XLA Modules:
  0.0 31.5 jit_solution(10786214504649761139)
XLA Ops:
  0.6 30.1 %shard_map.67 = (f32[2,512,128]{2,1,0:T(8,128)S(1)}, f32[2,512]{1,0:T(2,128)S(1)}, f32[2,1024]{1,0:T(2,128)S(1)}) custom-call(f32[3]{0:T(128)} %temp_in.1, bf16[1024,256]{1,0:T(8,128)(2,1)} %x_in.1, f32[2,512,128]{2,1,0:T(8,128)} %mu_in.1, f32[2,512]{1,0:T(2,128)} %lp_in.1), custom_call_target="tpu_custom_call" | custom-call | tf_op jit(solution)/shard_map/pallas_call | solution.py:403
  30.7 0.8 %shard_map.68 = (f32[2,512,128]{2,1,0:T(8,128)}, f32[2,512]{1,0:T(2,128)}, f32[2,1024]{1,0:T(2,128)}) custom-call(f32[2,512,128]{2,1,0:T(8,128)S(1)} %get-tuple-element.6.a, f32[2,512]{1,0:T(2,128)S(1)} %get-tuple-element.7.b, f32[2,1024]{1,0:T(2,128)S(1)} %get-tuple-element.8.c), custom_call_target="tpu_custom_call" | custom-call | tf_op jit(solution)/shard_map/pallas_call | solution.py:445

commit v4 on v3

--- a/solution.py
+++ b/solution.py
@@ -13,7 +13,10 @@
 LN2 = 0.6931471805599453
 LANES = 128
 TILE = 256
+FIRST = 8
+EARLY = 4
 PIECES = 4
+CROSSINGS = ((0, 7), (7, 7), (14, 2))
 
 MESH = pl.DeviceIdType.MESH
 F32 = jnp.float32
@@ -38,6 +41,7 @@
     mate = 2 * x + 1 - core
     across = 2 * (1 - x) + core
     across_mate = 2 * (1 - x) + 1 - core
+    across_one = 2 * (1 - x) + 1
 
     n_rows = xo.shape[0]
     n_comp = mub.shape[0]
@@ -53,6 +57,7 @@
     d_mate = {"row": mate}
     d_across = {"row": across}
     d_across_mate = {"row": across_mate}
+    d_across_one = {"row": across_one}
     d_y = {"comp": 1 - y}
     d_y_mate = {"comp": 1 - y, "row": mate}
 
@@ -66,38 +71,44 @@
         pltpu.make_async_copy(src, dst, s_in.at[i])
         for i, (src, dst) in enumerate((
             (x_in.at[:, other_col], xo),
-            (x_in.at[:, fit_col], xg.at[my_rows, :]),
-            (mu_in, mu0),
+            (mu_in.at[1 - x], mu0.at[1 - x]),
             (lp_in, lp0),
             (temp_in, temp_ref),
+            (x_in.at[:, fit_col], xg.at[my_rows, :]),
+            (mu_in.at[x], mu0.at[x]),
         ))
     ]
     barrier = pltpu.get_barrier_semaphore()
     for dev in (d_mate, d_across, d_across_mate, d_y, d_y_mate):
         pl.semaphore_signal(barrier, inc=1, device_id=dev, device_id_type=MESH)
-    for c in loads:
+    for c in loads[:4]:
         c.start()
     with jax.named_scope("barrier"):
         pl.semaphore_wait(barrier, 5)
+    for c in loads[4:]:
+        c.start()
     with jax.named_scope("loads"):
-        for c in loads:
+        for c in loads[:4]:
             c.wait()
 
     def rows_of(block, j):
         return pl.ds(pl.multiple_of(block * n_rows + j * TILE, TILE), TILE)
 
-    xs = [
-        remote(xo.at[pl.ds(j * TILE, TILE), :], xg.at[rows_of(row, j), :], s_x, r_x.at[j], d_across)
-        for j in range(tiles)
-    ]
-    relays = [
-        remote(xg.at[rows_of(across, j), :], xg.at[rows_of(across, j), :], s_rel, r_rel.at[j], d_mate)
-        for j in range(tiles)
-    ]
+    unit = n_rows // 16
+
+    def some_rows(block, p):
+        first, count = CROSSINGS[p]
+        return pl.ds(pl.multiple_of(block * n_rows + first * unit, unit), count * unit)
+
+    xs, relays = [], []
+    for p, (first, count) in enumerate(CROSSINGS):
+        xs.append(remote(xo.at[pl.ds(first * unit, count * unit), :], xg.at[some_rows(row, p), :],
+                         s_x, r_x.at[p], d_across))
+        got = xg.at[some_rows(across, p), :]
+        relays.append(remote(got, got, s_rel, r_rel, d_mate))
     own = remote(xg.at[my_rows, :], xg.at[my_rows, :], s_own, r_own, d_mate)
     for c in xs[:-1]:
         c.start()
-    own.start()
 
     def means_to(sweep, mean, logw, mub_at, cc_at):
         mub_at[...] = mean.astype(BF16)
@@ -124,19 +135,19 @@
             jnp.exp2(parts[2] - top) + jnp.exp2(parts[3] - top))
         return top + jnp.log2(tot)
 
-    def m_region(lses, base, pts, slot, n_at, s_at, first):
+    def m_region(lses, base, pts, at, n_at, s_at, first):
         ws = []
-        for j in range(tiles):
-            w = jnp.exp2(mm[base + j] - lses[j])
+        for j, lse in enumerate(lses):
+            w = jnp.exp2(mm[base + j] - lse)
             ws += [w[h:h + 1, :] for h in range(halves)]
         for k in range(0, n_comp, 16):
             acc = None if first else n_at[k:k + 16, :]
             for v, w in enumerate(ws):
                 r = ee[base + v // halves, k:k + 16, (v % halves) * LANES:(v % halves + 1) * LANES] * w
                 acc = r if acc is None else acc + r
-                rr[slot, k:k + 16, v * LANES:(v + 1) * LANES] = r.astype(BF16)
+                rr[k:k + 16, at + v * LANES:at + (v + 1) * LANES] = r.astype(BF16)
             n_at[k:k + 16, :] = acc
-        s = jnp.dot(rr[slot], pts, preferred_element_type=F32)
+        s = jnp.dot(rr[:, at:at + len(lses) * TILE], pts, preferred_element_type=F32)
         if first:
             s_at[...] = s
         else:
@@ -164,15 +175,19 @@
                     ahead = cross0(*order[i + 1])
                 e_tile(0, slot * tiles + j, a, cc0.at[slot], stats0.at[fo, 2 * y + slot % 2, j])
         st0_copy(fo).start()
+        if fo == 0:
+            for c in loads[4:]:
+                c.wait()
+            own.start()
 
     def part_copy(fo, k):
-        return remote(part.at[2 * fo, k], inbox.at[fo, k], s_part, r_part.at[fo, k], d_mate)
+        return remote(part.at[2 * fo, k], inbox.at[fo, k], s_part, r_part.at[2 if fo else k], d_mate)
 
     def m0(fo, qo):
         slot = 2 * fo + qo
         lses = [lse_of([stats0[fo, d, j] for d in range(4)]) for j in range(tiles)]
         pts = xg[my_rows, :] if fo else xo[...]
-        m_region(lses, slot * tiles, pts, slot, part.at[slot, 1], part.at[slot, 0], True)
+        m_region(lses, slot * tiles, pts, slot * n_rows, part.at[slot, 1], part.at[slot, 0], True)
 
     step = n_comp // PIECES
     with jax.named_scope("w_st0_0"):
@@ -188,7 +203,7 @@
     sums = []
     for p in range(PIECES):
         at = pl.ds(p * step, step)
-        xsend[at, :] = part[1, 0, at, :] + inbox[0, 0, at, :]
+        xsend[at, :] = (part[1, 0, at, :] + inbox[0, 0, at, :]).astype(BF16)
         c = remote(xsend.at[at, :], xin.at[at, :], s_xs, r_xs, d_across)
         c.start()
         sums.append(c)
@@ -207,54 +222,50 @@
         part_copy(1, k).start()
     with jax.named_scope("m0_3"):
         m0(1, 1)
-    for j in range(tiles - 1):
-        with jax.named_scope(f"w_x{j}"):
-            xs[j].wait_recv()
-        relays[j].start()
+    for p in range(len(xs) - 1):
+        with jax.named_scope(f"w_x{p}"):
+            xs[p].wait_recv()
+        relays[p].start()
     with jax.named_scope("w_part1"):
-        for k in range(2):
-            part_copy(1, k).wait_recv()
+        drain(inbox.at[1], r_part.at[2])
     with jax.named_scope("w_xin"):
         counts.wait_recv()
         drain(xsend, r_xs)
     n_across = column(jnp.concatenate([nin[h:h + 1, :] for h in range(n_comp // LANES)], axis=1))
-    ssum[...] = part[3, 0] + inbox[1, 0] + xin[...]
+    ssum[...] = part[3, 0] + inbox[1, 0] + xin[...].astype(F32)
     n_first = jnp.sum(part[3, 1] + inbox[1, 1], axis=1, keepdims=True) + n_across
 
-    def cross(block, j):
-        return lax.dot_general(mub[...], xg[rows_of(block, j), :], NT, preferred_element_type=F32)
-
-    def st_copy(sweep, block, k):
-        part = stats.at[sweep - 1, me, pl.ds(block * tiles, tiles)]
-        return remote(part, part, s_st, r_st.at[sweep - 1, block], (d_mate, d_y, d_y_mate)[k])
-
-    def send_stats(sweep, block):
-        for k in (1, 2, 0):
-            st_copy(sweep, block, k).start()
-
-    def e_blocks(sweep, todo):
-        order = [(block, j) for block in todo for j in range(tiles)]
-        ahead = cross(*order[0])
-        for i, (block, j) in enumerate(order):
+    def cross(t):
+        return lax.dot_general(mub[...], xg[pl.ds(pl.multiple_of(t * TILE, TILE), TILE), :], NT,
+                               preferred_element_type=F32)
+
+    def st_send(sweep, group):
+        t, count, sem = group
+        at = stats.at[sweep - 1, me, pl.ds(t, count)]
+        for dev in (d_y, d_y_mate, d_mate):
+            remote(at, at, s_st, r_st.at[sweep - 1, sem], dev).start()
+
+    def e_group(sweep, group):
+        t, count, _ = group
+        ahead = cross(t)
+        for i in range(count):
             a = ahead
-            if i + 1 < len(order):
-                ahead = cross(*order[i + 1])
-            t = block * tiles + j
-            e_tile(sweep, t, a, cc, stats.at[sweep - 1, me, t])
-            if j == tiles - 1:
-                send_stats(sweep, block)
-
-    def m_block(sweep, block, first):
+            if i + 1 < count:
+                ahead = cross(t + i + 1)
+            e_tile(sweep, t + i, a, cc, stats.at[sweep - 1, me, t + i])
+        st_send(sweep, group)
+
+    def m_group(sweep, t, count, sems, at, first):
         with jax.named_scope("stwait"):
-            drain(stats.at[sweep - 1, pl.ds(0, 3), pl.ds(block * tiles, tiles)], r_st.at[sweep - 1, block])
-        with jax.named_scope("mblock"):
+            for sem in sems:
+                drain(stats.at[sweep - 1, pl.ds(0, 3), pl.ds(0, count // len(sems))], r_st.at[sweep - 1, sem])
+        with jax.named_scope("mgroup"):
             lses = []
-            for j in range(tiles):
-                t = block * tiles + j
-                lses.append(lse_of([stats[sweep - 1, d, t] for d in range(4)]))
-                lse2[t] = lses[-1]
-            pts = xg[pl.ds(pl.multiple_of(block * n_rows, n_rows), n_rows), :]
-            m_region(lses, block * tiles, pts, block, nacc, ssum, first)
+            for j in range(count):
+                lses.append(lse_of([stats[sweep - 1, d, t + j] for d in range(4)]))
+                lse2[t + j] = lses[-1]
+            pts = xg[pl.ds(pl.multiple_of(t * TILE, TILE), count * TILE), :]
+            m_region(lses, t, pts, at, nacc, ssum, first)
 
     def finish(n):
         mean = ssum[...] / (n + EPS_COUNT)
@@ -266,44 +277,44 @@
         means_to(1, mean, logw, mub, cc)
     for sweep in range(1, sweeps):
         if sweep == 1:
-            with jax.named_scope("e_row"):
-                e_blocks(1, (row,))
+            near, far = 2 * x * tiles, 2 * (1 - x) * tiles
             with jax.named_scope("w_own"):
                 own.wait_recv()
-            with jax.named_scope("e_mate"):
-                e_blocks(1, (mate,))
+            with jax.named_scope("e_row_mate"):
+                e_group(1, (near, EARLY, 0))
             with jax.named_scope("w_x3"):
                 xs[-1].wait_recv()
             relays[-1].start()
+            if EARLY < 2 * tiles:
+                with jax.named_scope("e_row_mate2"):
+                    e_group(1, (near + EARLY, 2 * tiles - EARLY, 3))
             with jax.named_scope("e_across"):
-                e_blocks(1, (across,))
+                e_group(1, (across * tiles, tiles, 1 + core))
             with jax.named_scope("w_rel"):
-                for c in relays:
-                    c.wait_recv()
+                drain(xo, r_rel)
             with jax.named_scope("e_across_mate"):
-                e_blocks(1, (across_mate,))
-            order = (row, mate, across, across_mate)
+                e_group(1, (across_mate * tiles, tiles, 2 - core))
+            m_group(1, near, 2 * tiles, (0, 3) if EARLY < 2 * tiles else (0,), 0, True)
+            m_group(1, far, 2 * tiles, (1, 2), 2 * n_rows, False)
         else:
+            n_tiles = blocks * tiles
             with jax.named_scope("esweep"):
-                e_blocks(sweep, range(blocks))
-            order = range(blocks)
-        for i, block in enumerate(order):
-            m_block(sweep, block, i == 0)
+                e_group(sweep, (0, FIRST, 0))
+                e_group(sweep, (FIRST, n_tiles - FIRST, 1))
+            m_group(sweep, 0, FIRST, (0,), 0, True)
+            m_group(sweep, FIRST, n_tiles - FIRST, (1,), FIRST * TILE, False)
         with jax.named_scope("finish"):
             mean, logw = finish(jnp.sum(nacc[...], axis=1, keepdims=True))
             if sweep + 1 < sweeps:
                 means_to(sweep + 1, mean, logw, mub, cc)
 
     mu_out[x, my_comps, :] = mean
-    fins = []
-
-    def piece(fit, p):
-        return mu_out.at[fit, pl.ds(pl.multiple_of(core * n_comp + p * step, step), step), :]
+
+    def piece(fit, one, p):
+        return mu_out.at[fit, pl.ds(pl.multiple_of(one * n_comp + p * step, step), step), :]
 
     for p in range(PIECES):
-        c = remote(piece(x, p), piece(x, p), s_fin, r_fin.at[p], d_across)
-        c.start()
-        fins.append(c)
+        remote(piece(x, core, p), piece(x, core, p), s_fin, r_fin.at[core, p], d_across_one).start()
     whole = mu_out.at[x, my_comps, :]
     to_mate = remote(whole, whole, s_mate, r_mate, d_mate)
     to_mate.start()
@@ -340,13 +351,15 @@
     with jax.named_scope("lse"):
         sq_own = sq_rows(xg[my_rows, :])
         sq_other = sq_rows(xo[...])
-    frels = []
-    for p in range(PIECES):
-        with jax.named_scope(f"w_fin{p}"):
-            fins[p].wait_recv()
-        c = remote(piece(1 - x, p), piece(1 - x, p), s_frl, r_frl, d_mate)
-        c.start()
-        frels.append(c)
+    @pl.when(core == 1)
+    def _():
+        for p in range(PIECES):
+            for one in (1, 0):
+                got = piece(1 - x, one, p)
+                with jax.named_scope(f"w_fin{p}{one}"):
+                    remote(got, got, s_fin, r_fin.at[one, p], d_across).wait_recv()
+                remote(got, got, s_frl, r_frl, d_mate).start()
+
     with jax.named_scope("w_last"):
         last.wait_recv()
     write_lse(sq_own, sq_other)
@@ -357,7 +370,11 @@
             lp_out[b // 2:b // 2 + 1, at:at + LANES] = aux[b, h:h + 1, :]
     with jax.named_scope("w_frel"):
         to_mate.wait_recv()
-        drain(ssum, r_frl)
+
+        @pl.when(core == 0)
+        def _():
+            drain(mu_out.at[0], r_frl)
+
     with jax.named_scope("w_sends"):
         for c in (own, to_mate, last, counts):
             c.wait_send()
@@ -367,7 +384,11 @@
         drain(xo, s_x)
         drain(xo, s_rel)
         drain(ssum, s_fin)
-        drain(ssum, s_frl)
+
+        @pl.when(core == 1)
+        def _():
+            drain(mu_out.at[0], s_frl)
+
         drain(aux.at[pl.ds(0, 3)], s_aux)
         drain(stats.at[:, pl.ds(0, 3)], s_st)
 
@@ -420,8 +441,8 @@
                 pltpu.VMEM((2, 4, tiles, halves, LANES), F32),
                 pltpu.VMEM((4, 2, n_comp, LANES), F32),
                 pltpu.VMEM((2, 2, n_comp, LANES), F32),
-                pltpu.VMEM((n_comp, half), F32),
-                pltpu.VMEM((n_comp, half), F32),
+                pltpu.VMEM((n_comp, half), BF16),
+                pltpu.VMEM((n_comp, half), BF16),
                 pltpu.VMEM((n_comp // LANES, LANES), F32),
                 pltpu.VMEM((n_comp // LANES, LANES), F32),
                 pltpu.VMEM((n_comp, half), BF16),
@@ -429,15 +450,15 @@
                 pltpu.VMEM((n_tiles, n_comp, TILE), F32),
                 pltpu.VMEM((n_tiles, halves, LANES), F32),
                 pltpu.VMEM((sweeps - 1, 4, n_tiles, halves, LANES), F32),
-                pltpu.VMEM((rows_size, n_comp, n_rows), BF16),
+                pltpu.VMEM((n_comp, total_pts), BF16),
                 pltpu.VMEM((n_comp, half), F32),
                 pltpu.VMEM((n_comp, LANES), F32),
                 pltpu.VMEM((n_tiles, halves, LANES), F32),
                 pltpu.VMEM((tiles, halves, LANES), F32),
                 pltpu.VMEM((rows_size, n_comp // LANES, LANES), F32),
-                dma((5,)), dma, dma, dma, dma((tiles,)), dma, dma((tiles,)), dma, dma((2,)), dma, dma((2, 2)),
-                dma, dma, dma, dma, dma, dma((sweeps - 1, rows_size)), dma, dma,
-                dma, dma((PIECES,)), dma, dma, dma, dma, dma, dma,
+                dma((6,)), dma, dma, dma, dma((len(CROSSINGS),)), dma, dma, dma, dma((2,)), dma, dma((3,)),
+                dma, dma, dma, dma, dma, dma((sweeps - 1, 4)), dma, dma,
+                dma, dma((2, PIECES)), dma, dma, dma, dma, dma, dma,
             ],
             compiler_params=pltpu.CompilerParams(collective_id=0, has_side_effects=True),
         )(inv_temp, x_local, mu_init, logpi_init)

time: 31.6 us -> 29.9 us (0.946)
  Pallas kernels: 30.9 us -> 29.2 us
    pallas_call x1, Pallas kernels: 30.1 us -> 28.3 us  [local_fit(): pl.pallas_call(functools.partial(em_kernel, sweeps, total_pts, n_half * c...]
where the time goes in v4:
time: 29.9 us; the launch traced here: 29.8 us
  Pallas kernels  29.2 us (98%)
  between operations  0.64 us (2%)
    pallas_call x1, Pallas kernels, local_fit(): pl.pallas_call(functools.partial(em_kernel, sweeps, total_pts, n_half * c...  28.3 us
    pallas_call x1, Pallas kernels, local_fit(): pl.pallas_call(store_kernel, out_shape=tuple((jax.ShapeDtypeStruct(o.shap...  0.83 us

profile of v4, /device:TPU:0, one launch (start us, length us, event | category | flops | bytes accessed | tf_op | source)
XLA Modules:
  0.0 29.8 jit_solution(16180097453792804222)
XLA Ops:
  0.6 28.3 %shard_map.67 = (f32[2,512,128]{2,1,0:T(8,128)S(1)}, f32[2,512]{1,0:T(2,128)S(1)}, f32[2,1024]{1,0:T(2,128)S(1)}) custom-call(f32[3]{0:T(128)} %temp_in.1, bf16[1024,256]{1,0:T(8,128)(2,1)} %x_in.1, f32[2,512,128]{2,1,0:T(8,128)} %mu_in.1, f32[2,512]{1,0:T(2,128)} %lp_in.1), custom_call_target="tpu_custom_call" | custom-call | tf_op jit(solution)/shard_map/pallas_call | solution.py:424
  29.0 0.8 %shard_map.68 = (f32[2,512,128]{2,1,0:T(8,128)}, f32[2,512]{1,0:T(2,128)}, f32[2,1024]{1,0:T(2,128)}) custom-call(f32[2,512,128]{2,1,0:T(8,128)S(1)} %get-tuple-element.6.a, f32[2,512]{1,0:T(2,128)S(1)} %get-tuple-element.7.b, f32[2,1024]{1,0:T(2,128)S(1)} %get-tuple-element.8.c), custom_call_target="tpu_custom_call" | custom-call | tf_op jit(solution)/shard_map/pallas_call | solution.py:466

commit v5 on v4

--- a/solution.py
+++ b/solution.py
@@ -16,7 +16,7 @@
 FIRST = 8
 EARLY = 4
 PIECES = 4
-CROSSINGS = ((0, 7), (7, 7), (14, 2))
+CROSSINGS = ((0, 7), (7, 8), (15, 1))
 
 MESH = pl.DeviceIdType.MESH
 F32 = jnp.float32
@@ -30,8 +30,7 @@
     mu_out, lp_out, lse_out,
     temp_ref, xo, xg, mu0, lp0, mub0, cc0, stats0, part, inbox, xsend, xin, nsend, nin,
     mub, cc, ee, mm, stats, rr, ssum, nacc, lse2, lse_in, aux,
-    s_in, s_own, r_own, s_x, r_x, s_rel, r_rel, s_st0, r_st0, s_part, r_part, s_xs, r_xs, s_n, r_n,
-    s_st, r_st, s_lse, r_lse, s_fin, r_fin, s_mate, r_mate, s_frl, r_frl, s_aux, r_aux,
+    s_in, s_out, r_own, r_x, r_rel, r_st0, r_part, r_xs, r_n, r_st, r_lse, r_fin, r_mate, r_frl, r_aux,
 ):
     row = lax.axis_index("row")
     y = lax.axis_index("comp")
@@ -88,8 +87,7 @@
     for c in loads[4:]:
         c.start()
     with jax.named_scope("loads"):
-        for c in loads[:4]:
-            c.wait()
+        loads[0].wait()
 
     def rows_of(block, j):
         return pl.ds(pl.multiple_of(block * n_rows + j * TILE, TILE), TILE)
@@ -103,12 +101,14 @@
     xs, relays = [], []
     for p, (first, count) in enumerate(CROSSINGS):
         xs.append(remote(xo.at[pl.ds(first * unit, count * unit), :], xg.at[some_rows(row, p), :],
-                         s_x, r_x.at[p], d_across))
+                         s_out, r_x.at[p], d_across))
         got = xg.at[some_rows(across, p), :]
-        relays.append(remote(got, got, s_rel, r_rel, d_mate))
-    own = remote(xg.at[my_rows, :], xg.at[my_rows, :], s_own, r_own, d_mate)
+        relays.append(remote(got, got, s_out, r_rel.at[int(p == len(CROSSINGS) - 1)], d_mate))
+    own = remote(xg.at[my_rows, :], xg.at[my_rows, :], s_out, r_own, d_mate)
     for c in xs[:-1]:
         c.start()
+    for c in loads[1:4]:
+        c.wait()
 
     def means_to(sweep, mean, logw, mub_at, cc_at):
         mub_at[...] = mean.astype(BF16)
@@ -135,23 +135,23 @@
             jnp.exp2(parts[2] - top) + jnp.exp2(parts[3] - top))
         return top + jnp.log2(tot)
 
-    def m_region(lses, base, pts, at, n_at, s_at, first):
+    def m_region(lses, base, pts, at, n_at, s_at, first, lo=0, hi=n_comp):
         ws = []
         for j, lse in enumerate(lses):
             w = jnp.exp2(mm[base + j] - lse)
             ws += [w[h:h + 1, :] for h in range(halves)]
-        for k in range(0, n_comp, 16):
+        for k in range(lo, hi, 16):
             acc = None if first else n_at[k:k + 16, :]
             for v, w in enumerate(ws):
                 r = ee[base + v // halves, k:k + 16, (v % halves) * LANES:(v % halves + 1) * LANES] * w
                 acc = r if acc is None else acc + r
                 rr[k:k + 16, at + v * LANES:at + (v + 1) * LANES] = r.astype(BF16)
             n_at[k:k + 16, :] = acc
-        s = jnp.dot(rr[:, at:at + len(lses) * TILE], pts, preferred_element_type=F32)
+        s = jnp.dot(rr[lo:hi, at:at + len(lses) * TILE], pts, preferred_element_type=F32)
         if first:
-            s_at[...] = s
+            s_at[lo:hi, :] = s
         else:
-            s_at[...] += s
+            s_at[lo:hi, :] += s
 
     def cross0(slot, j):
         pts = xg[rows_of(row, j), :] if slot // 2 else xo[pl.ds(j * TILE, TILE), :]
@@ -159,7 +159,7 @@
 
     def st0_copy(fo):
         at = stats0.at[fo, pl.ds(2 * y, 2)]
-        return remote(at, at, s_st0, r_st0.at[fo], d_y)
+        return remote(at, at, s_out, r_st0.at[fo], d_y)
 
     for fo, fit in enumerate((1 - x, x)):
         with jax.named_scope(f"set0_{fo}"):
@@ -181,7 +181,7 @@
             own.start()
 
     def part_copy(fo, k):
-        return remote(part.at[2 * fo, k], inbox.at[fo, k], s_part, r_part.at[2 if fo else k], d_mate)
+        return remote(part.at[2 * fo, k], inbox.at[fo, k], s_out, r_part.at[2 if fo else k], d_mate)
 
     def m0(fo, qo):
         slot = 2 * fo + qo
@@ -204,14 +204,14 @@
     for p in range(PIECES):
         at = pl.ds(p * step, step)
         xsend[at, :] = (part[1, 0, at, :] + inbox[0, 0, at, :]).astype(BF16)
-        c = remote(xsend.at[at, :], xin.at[at, :], s_xs, r_xs, d_across)
+        c = remote(xsend.at[at, :], xin.at[at, :], s_out, r_xs, d_across)
         c.start()
         sums.append(c)
     part_copy(0, 1).wait_recv()
     flat = jnp.sum(jnp.transpose(part[1, 1] + inbox[0, 1]), axis=0, keepdims=True)
     for h in range(n_comp // LANES):
         nsend[h:h + 1, :] = flat[:, h * LANES:(h + 1) * LANES]
-    counts = remote(nsend, nin, s_n, r_n, d_across)
+    counts = remote(nsend, nin, s_out, r_n, d_across)
     counts.start()
     xs[-1].start()
     with jax.named_scope("w_st0_1"):
@@ -240,22 +240,23 @@
                                preferred_element_type=F32)
 
     def st_send(sweep, group):
-        t, count, sem = group
+        t, count, sem = group[:3]
         at = stats.at[sweep - 1, me, pl.ds(t, count)]
         for dev in (d_y, d_y_mate, d_mate):
-            remote(at, at, s_st, r_st.at[sweep - 1, sem], dev).start()
-
-    def e_group(sweep, group):
-        t, count, _ = group
-        ahead = cross(t)
-        for i in range(count):
+            remote(at, at, s_out, r_st.at[sweep - 1, sem], dev).start()
+
+    def e_group(sweep, *groups):
+        todo = [t + i for t, count, _ in groups for i in range(count)]
+        ahead = cross(todo[0])
+        for i, t in enumerate(todo):
             a = ahead
-            if i + 1 < count:
-                ahead = cross(t + i + 1)
-            e_tile(sweep, t + i, a, cc, stats.at[sweep - 1, me, t + i])
-        st_send(sweep, group)
-
-    def m_group(sweep, t, count, sems, at, first):
+            if i + 1 < len(todo):
+                ahead = cross(todo[i + 1])
+            e_tile(sweep, t, a, cc, stats.at[sweep - 1, me, t])
+        for group in groups:
+            st_send(sweep, group)
+
+    def m_group(sweep, t, count, sems, at, first, after=None):
         with jax.named_scope("stwait"):
             for sem in sems:
                 drain(stats.at[sweep - 1, pl.ds(0, 3), pl.ds(0, count // len(sems))], r_st.at[sweep - 1, sem])
@@ -265,12 +266,26 @@
                 lses.append(lse_of([stats[sweep - 1, d, t + j] for d in range(4)]))
                 lse2[t + j] = lses[-1]
             pts = xg[pl.ds(pl.multiple_of(t * TILE, TILE), count * TILE), :]
-            m_region(lses, t, pts, at, nacc, ssum, first)
+            if after is None:
+                m_region(lses, t, pts, at, nacc, ssum, first)
+            else:
+                for lo in range(0, n_comp, n_comp // 2):
+                    m_region(lses, t, pts, at, nacc, ssum, first, lo, lo + n_comp // 2)
+                    after(lo, lo + n_comp // 2)
 
     def finish(n):
         mean = ssum[...] / (n + EPS_COUNT)
         logw = jnp.log((n + PRIOR_ALPHA) / (total_pts + total_comp * PRIOR_ALPHA))
         return mean, logw
+
+    def piece(fit, one, p):
+        return mu_out.at[fit, pl.ds(pl.multiple_of(one * n_comp + p * step, step), step), :]
+
+    def send_final(lo, hi):
+        n = jnp.sum(nacc[lo:hi, :], axis=1, keepdims=True)
+        mu_out[x, pl.ds(pl.multiple_of(core * n_comp + lo, step), hi - lo), :] = ssum[lo:hi, :] / (n + EPS_COUNT)
+        for p in range(lo // step, hi // step):
+            remote(piece(x, core, p), piece(x, core, p), s_out, r_fin.at[p], d_across_one).start()
 
     with jax.named_scope("finish"):
         mean, logw = finish(n_first)
@@ -288,44 +303,42 @@
             if EARLY < 2 * tiles:
                 with jax.named_scope("e_row_mate2"):
                     e_group(1, (near + EARLY, 2 * tiles - EARLY, 3))
-            with jax.named_scope("e_across"):
-                e_group(1, (across * tiles, tiles, 1 + core))
+            most = tiles - 1
             with jax.named_scope("w_rel"):
-                drain(xo, r_rel)
-            with jax.named_scope("e_across_mate"):
-                e_group(1, (across_mate * tiles, tiles, 2 - core))
+                drain(xg.at[pl.ds(0, (CROSSINGS[-1][0] * n_rows) // 16), :], r_rel.at[0])
+            with jax.named_scope("e_far"):
+                e_group(1, (across * tiles, most, 1), (across_mate * tiles, most, 1))
+            with jax.named_scope("w_rel"):
+                drain(xg.at[pl.ds(0, (CROSSINGS[-1][1] * n_rows) // 16), :], r_rel.at[1])
+            with jax.named_scope("e_far2"):
+                e_group(1, (across * tiles + most, 1, 1), (across_mate * tiles + most, 1, 1))
             m_group(1, near, 2 * tiles, (0, 3) if EARLY < 2 * tiles else (0,), 0, True)
-            m_group(1, far, 2 * tiles, (1, 2), 2 * n_rows, False)
+            m_group(1, far, 2 * tiles, (1,), 2 * n_rows, False)
         else:
             n_tiles = blocks * tiles
             with jax.named_scope("esweep"):
                 e_group(sweep, (0, FIRST, 0))
                 e_group(sweep, (FIRST, n_tiles - FIRST, 1))
             m_group(sweep, 0, FIRST, (0,), 0, True)
-            m_group(sweep, FIRST, n_tiles - FIRST, (1,), FIRST * TILE, False)
-        with jax.named_scope("finish"):
-            mean, logw = finish(jnp.sum(nacc[...], axis=1, keepdims=True))
-            if sweep + 1 < sweeps:
+            m_group(sweep, FIRST, n_tiles - FIRST, (1,), FIRST * TILE, False,
+                    send_final if sweep == sweeps - 1 else None)
+        if sweep < sweeps - 1:
+            with jax.named_scope("finish"):
+                mean, logw = finish(jnp.sum(nacc[...], axis=1, keepdims=True))
                 means_to(sweep + 1, mean, logw, mub, cc)
 
-    mu_out[x, my_comps, :] = mean
-
-    def piece(fit, one, p):
-        return mu_out.at[fit, pl.ds(pl.multiple_of(one * n_comp + p * step, step), step), :]
-
-    for p in range(PIECES):
-        remote(piece(x, core, p), piece(x, core, p), s_fin, r_fin.at[core, p], d_across_one).start()
     whole = mu_out.at[x, my_comps, :]
-    to_mate = remote(whole, whole, s_mate, r_mate, d_mate)
+    to_mate = remote(whole, whole, s_out, r_mate, d_mate)
     to_mate.start()
-    last = remote(lse2.at[pl.ds(across * tiles, tiles)], lse_in, s_lse, r_lse, d_across)
+    last = remote(lse2.at[pl.ds(across * tiles, tiles)], lse_in, s_out, r_lse, d_across)
     last.start()
-    flat = jnp.transpose(jnp.broadcast_to(logw, (n_comp, LANES)))[0:1, :]
+    n_last = jnp.sum(jnp.transpose(nacc[...]), axis=0, keepdims=True)
+    flat = jnp.log((n_last + PRIOR_ALPHA) / (total_pts + total_comp * PRIOR_ALPHA))
     for h in range(n_comp // LANES):
         aux[row, h:h + 1, :] = flat[:, h * LANES:(h + 1) * LANES]
     auxs = []
     for k, dev in enumerate((d_mate, d_across, d_across_mate)):
-        c = remote(aux.at[row], aux.at[row], s_aux, r_aux, dev)
+        c = remote(aux.at[row], aux.at[row], s_out, r_aux, dev)
         c.start()
         auxs.append(c)
 
@@ -354,11 +367,11 @@
     @pl.when(core == 1)
     def _():
         for p in range(PIECES):
-            for one in (1, 0):
+            with jax.named_scope(f"w_fin{p}"):
+                drain(ssum.at[pl.ds(0, 2 * step)], r_fin.at[p])
+            for one in range(2):
                 got = piece(1 - x, one, p)
-                with jax.named_scope(f"w_fin{p}{one}"):
-                    remote(got, got, s_fin, r_fin.at[one, p], d_across).wait_recv()
-                remote(got, got, s_frl, r_frl, d_mate).start()
+                remote(got, got, s_out, r_frl, d_mate).start()
 
     with jax.named_scope("w_last"):
         last.wait_recv()
@@ -378,19 +391,19 @@
     with jax.named_scope("w_sends"):
         for c in (own, to_mate, last, counts):
             c.wait_send()
-        drain(stats0.at[:, pl.ds(0, 2)], s_st0)
-        drain(part.at[pl.ds(0, 2)], s_part)
-        drain(xsend, s_xs)
-        drain(xo, s_x)
-        drain(xo, s_rel)
-        drain(ssum, s_fin)
+        drain(stats0.at[:, pl.ds(0, 2)], s_out)
+        drain(part.at[pl.ds(0, 2)], s_out)
+        drain(xsend, s_out)
+        drain(xo, s_out)
+        drain(xo, s_out)
+        drain(ssum, s_out)
 
         @pl.when(core == 1)
         def _():
-            drain(mu_out.at[0], s_frl)
-
-        drain(aux.at[pl.ds(0, 3)], s_aux)
-        drain(stats.at[:, pl.ds(0, 3)], s_st)
+            drain(mu_out.at[0], s_out)
+
+        drain(aux.at[pl.ds(0, 3)], s_out)
+        drain(stats.at[:, pl.ds(0, 3)], s_out)
 
 
 def store_kernel(a, b, c, a_out, b_out, c_out, sem):
@@ -456,9 +469,8 @@
                 pltpu.VMEM((n_tiles, halves, LANES), F32),
                 pltpu.VMEM((tiles, halves, LANES), F32),
                 pltpu.VMEM((rows_size, n_comp // LANES, LANES), F32),
-                dma((6,)), dma, dma, dma, dma((len(CROSSINGS),)), dma, dma, dma, dma((2,)), dma, dma((3,)),
-                dma, dma, dma, dma, dma, dma((sweeps - 1, 4)), dma, dma,
-                dma, dma((2, PIECES)), dma, dma, dma, dma, dma, dma,
+                dma((6,)), dma, dma, dma((len(CROSSINGS),)), dma((2,)), dma((2,)), dma((3,)), dma, dma,
+                dma((sweeps - 1, 4)), dma, dma((PIECES,)), dma, dma, dma,
             ],
             compiler_params=pltpu.CompilerParams(collective_id=0, has_side_effects=True),
         )(inv_temp, x_local, mu_init, logpi_init)

time: 29.9 us -> 29.3 us (0.980)
  Pallas kernels: 29.2 us -> 28.6 us
    pallas_call x1, Pallas kernels: 28.3 us -> 27.8 us  [local_fit(): pl.pallas_call(functools.partial(em_kernel, sweeps, total_pts, n_half * c...]
where the time goes in v5:
time: 29.3 us; the launch traced here: 29.2 us
  Pallas kernels  28.6 us (98%)
  between operations  0.64 us (2%)
    pallas_call x1, Pallas kernels, local_fit(): pl.pallas_call(functools.partial(em_kernel, sweeps, total_pts, n_half * c...  27.8 us
    pallas_call x1, Pallas kernels, local_fit(): pl.pallas_call(store_kernel, out_shape=tuple((jax.ShapeDtypeStruct(o.shap...  0.83 us

profile of v5, /device:TPU:0, one launch (start us, length us, event | category | flops | bytes accessed | tf_op | source)
XLA Modules:
  0.0 29.2 jit_solution(11067694702237370021)
XLA Ops:
  0.6 27.8 %shard_map.67 = (f32[2,512,128]{2,1,0:T(8,128)S(1)}, f32[2,512]{1,0:T(2,128)S(1)}, f32[2,1024]{1,0:T(2,128)S(1)}) custom-call(f32[3]{0:T(128)} %temp_in.1, bf16[1024,256]{1,0:T(8,128)(2,1)} %x_in.1, f32[2,512,128]{2,1,0:T(8,128)} %mu_in.1, f32[2,512]{1,0:T(2,128)} %lp_in.1), custom_call_target="tpu_custom_call" | custom-call | tf_op jit(solution)/shard_map/pallas_call | solution.py:437
  28.4 0.8 %shard_map.68 = (f32[2,512,128]{2,1,0:T(8,128)}, f32[2,512]{1,0:T(2,128)}, f32[2,1024]{1,0:T(2,128)}) custom-call(f32[2,512,128]{2,1,0:T(8,128)S(1)} %get-tuple-element.6.a, f32[2,512]{1,0:T(2,128)S(1)} %get-tuple-element.7.b, f32[2,1024]{1,0:T(2,128)S(1)} %get-tuple-element.8.c), custom_call_target="tpu_custom_call" | custom-call | tf_op jit(solution)/shard_map/pallas_call | solution.py:478

commit v6 on v5

--- a/solution.py
+++ b/solution.py
@@ -14,9 +14,8 @@
 LANES = 128
 TILE = 256
 FIRST = 8
-EARLY = 4
 PIECES = 4
-CROSSINGS = ((0, 7), (7, 8), (15, 1))
+SHARED = 3
 
 MESH = pl.DeviceIdType.MESH
 F32 = jnp.float32
@@ -30,7 +29,7 @@
     mu_out, lp_out, lse_out,
     temp_ref, xo, xg, mu0, lp0, mub0, cc0, stats0, part, inbox, xsend, xin, nsend, nin,
     mub, cc, ee, mm, stats, rr, ssum, nacc, lse2, lse_in, aux,
-    s_in, s_out, r_own, r_x, r_rel, r_st0, r_part, r_xs, r_n, r_st, r_lse, r_fin, r_mate, r_frl, r_aux,
+    s_in, s_out, r_own, r_x, r_y, r_rel, r_st0, r_part, r_xs, r_n, r_st, r_lse, r_fin, r_mate, r_frl, r_aux,
 ):
     row = lax.axis_index("row")
     y = lax.axis_index("comp")
@@ -93,19 +92,25 @@
         return pl.ds(pl.multiple_of(block * n_rows + j * TILE, TILE), TILE)
 
     unit = n_rows // 16
-
-    def some_rows(block, p):
-        first, count = CROSSINGS[p]
+    both = 16 - 2 * SHARED
+    once = both + SHARED * y
+    chunks = ((once, SHARED), (0, both // 2), (both // 2, both - both // 2))
+
+    def some_rows(block, first, count):
         return pl.ds(pl.multiple_of(block * n_rows + first * unit, unit), count * unit)
 
     xs, relays = [], []
-    for p, (first, count) in enumerate(CROSSINGS):
-        xs.append(remote(xo.at[pl.ds(first * unit, count * unit), :], xg.at[some_rows(row, p), :],
+    for p, (first, count) in enumerate(chunks):
+        xs.append(remote(xo.at[some_rows(0, first, count), :], xg.at[some_rows(row, first, count), :],
                          s_out, r_x.at[p], d_across))
-        got = xg.at[some_rows(across, p), :]
-        relays.append(remote(got, got, s_out, r_rel.at[int(p == len(CROSSINGS) - 1)], d_mate))
+        got = xg.at[some_rows(across, first, count), :]
+        relays.append(remote(got, got, s_out, r_rel, d_mate))
+    got = xg.at[some_rows(across, once, SHARED), :]
+    over_y = remote(got, got, s_out, r_y, d_y)
+    got = xg.at[some_rows(across, both + SHARED * (1 - y), SHARED), :]
+    relays.append(remote(got, got, s_out, r_rel, d_mate))
     own = remote(xg.at[my_rows, :], xg.at[my_rows, :], s_out, r_own, d_mate)
-    for c in xs[:-1]:
+    for c in xs:
         c.start()
     for c in loads[1:4]:
         c.wait()
@@ -198,6 +203,10 @@
         part_copy(0, k).start()
     with jax.named_scope("m0_1"):
         m0(0, 1)
+    with jax.named_scope("w_x0"):
+        xs[0].wait_recv()
+    over_y.start()
+    relays[0].start()
     with jax.named_scope("w_part0"):
         part_copy(0, 0).wait_recv()
     sums = []
@@ -213,7 +222,6 @@
         nsend[h:h + 1, :] = flat[:, h * LANES:(h + 1) * LANES]
     counts = remote(nsend, nin, s_out, r_n, d_across)
     counts.start()
-    xs[-1].start()
     with jax.named_scope("w_st0_1"):
         st0_copy(1).wait_recv()
     with jax.named_scope("m0_2"):
@@ -222,12 +230,15 @@
         part_copy(1, k).start()
     with jax.named_scope("m0_3"):
         m0(1, 1)
-    for p in range(len(xs) - 1):
+    for p in range(1, len(xs)):
         with jax.named_scope(f"w_x{p}"):
             xs[p].wait_recv()
         relays[p].start()
     with jax.named_scope("w_part1"):
         drain(inbox.at[1], r_part.at[2])
+    with jax.named_scope("w_y"):
+        over_y.wait_recv()
+    relays[-1].start()
     with jax.named_scope("w_xin"):
         counts.wait_recv()
         drain(xsend, r_xs)
@@ -295,24 +306,13 @@
             near, far = 2 * x * tiles, 2 * (1 - x) * tiles
             with jax.named_scope("w_own"):
                 own.wait_recv()
-            with jax.named_scope("e_row_mate"):
-                e_group(1, (near, EARLY, 0))
-            with jax.named_scope("w_x3"):
-                xs[-1].wait_recv()
-            relays[-1].start()
-            if EARLY < 2 * tiles:
-                with jax.named_scope("e_row_mate2"):
-                    e_group(1, (near + EARLY, 2 * tiles - EARLY, 3))
-            most = tiles - 1
+            with jax.named_scope("e_near"):
+                e_group(1, (near, 2 * tiles, 0))
             with jax.named_scope("w_rel"):
-                drain(xg.at[pl.ds(0, (CROSSINGS[-1][0] * n_rows) // 16), :], r_rel.at[0])
+                drain(xo, r_rel)
             with jax.named_scope("e_far"):
-                e_group(1, (across * tiles, most, 1), (across_mate * tiles, most, 1))
-            with jax.named_scope("w_rel"):
-                drain(xg.at[pl.ds(0, (CROSSINGS[-1][1] * n_rows) // 16), :], r_rel.at[1])
-            with jax.named_scope("e_far2"):
-                e_group(1, (across * tiles + most, 1, 1), (across_mate * tiles + most, 1, 1))
-            m_group(1, near, 2 * tiles, (0, 3) if EARLY < 2 * tiles else (0,), 0, True)
+                e_group(1, (far, 2 * tiles, 1))
+            m_group(1, near, 2 * tiles, (0,), 0, True)
             m_group(1, far, 2 * tiles, (1,), 2 * n_rows, False)
         else:
             n_tiles = blocks * tiles
@@ -389,12 +389,12 @@
             drain(mu_out.at[0], r_frl)
 
     with jax.named_scope("w_sends"):
-        for c in (own, to_mate, last, counts):
+        for c in (own, to_mate, last, counts, over_y):
             c.wait_send()
         drain(stats0.at[:, pl.ds(0, 2)], s_out)
         drain(part.at[pl.ds(0, 2)], s_out)
         drain(xsend, s_out)
-        drain(xo, s_out)
+        drain(xo.at[pl.ds(0, (both + SHARED) * unit), :], s_out)
         drain(xo, s_out)
         drain(ssum, s_out)
 
@@ -469,8 +469,8 @@
                 pltpu.VMEM((n_tiles, halves, LANES), F32),
                 pltpu.VMEM((tiles, halves, LANES), F32),
                 pltpu.VMEM((rows_size, n_comp // LANES, LANES), F32),
-                dma((6,)), dma, dma, dma((len(CROSSINGS),)), dma((2,)), dma((2,)), dma((3,)), dma, dma,
-                dma((sweeps - 1, 4)), dma, dma((PIECES,)), dma, dma, dma,
+                dma((6,)), dma, dma, dma((3,)), dma, dma, dma((2,)), dma((3,)), dma, dma,
+                dma((sweeps - 1, 2)), dma, dma((PIECES,)), dma, dma, dma,
             ],
             compiler_params=pltpu.CompilerParams(collective_id=0, has_side_effects=True),
         )(inv_temp, x_local, mu_init, logpi_init)

time: 29.3 us -> 28.9 us (0.986)
  Pallas kernels: 28.6 us -> 28.1 us
    pallas_call x1, Pallas kernels: 27.8 us -> 27.3 us  [local_fit(): pl.pallas_call(functools.partial(em_kernel, sweeps, total_pts, n_half * c...]
where the time goes in v6:
time: 28.9 us; the launch traced here: 28.7 us
  Pallas kernels  28.1 us (97%)
  between operations  0.64 us (2%)
    pallas_call x1, Pallas kernels, local_fit(): pl.pallas_call(functools.partial(em_kernel, sweeps, total_pts, n_half * c...  27.3 us
    pallas_call x1, Pallas kernels, local_fit(): pl.pallas_call(store_kernel, out_shape=tuple((jax.ShapeDtypeStruct(o.shap...  0.83 us

profile of v6, /device:TPU:0, one launch (start us, length us, event | category | flops | bytes accessed | tf_op | source)
XLA Modules:
  0.0 28.7 jit_solution(4899977325823124819)
XLA Ops:
  0.6 27.3 %shard_map.67 = (f32[2,512,128]{2,1,0:T(8,128)S(1)}, f32[2,512]{1,0:T(2,128)S(1)}, f32[2,1024]{1,0:T(2,128)S(1)}) custom-call(f32[3]{0:T(128)} %temp_in.1, bf16[1024,256]{1,0:T(8,128)(2,1)} %x_in.1, f32[2,512,128]{2,1,0:T(8,128)} %mu_in.1, f32[2,512]{1,0:T(2,128)} %lp_in.1), custom_call_target="tpu_custom_call" | custom-call | tf_op jit(solution)/shard_map/pallas_call | solution.py:437
  27.9 0.8 %shard_map.68 = (f32[2,512,128]{2,1,0:T(8,128)}, f32[2,512]{1,0:T(2,128)}, f32[2,1024]{1,0:T(2,128)}) custom-call(f32[2,512,128]{2,1,0:T(8,128)S(1)} %get-tuple-element.6.a, f32[2,512]{1,0:T(2,128)S(1)} %get-tuple-element.7.b, f32[2,1024]{1,0:T(2,128)S(1)} %get-tuple-element.8.c), custom_call_target="tpu_custom_call" | custom-call | tf_op jit(solution)/shard_map/pallas_call | solution.py:478

commit v7 on v6

--- a/solution.py
+++ b/solution.py
@@ -13,8 +13,8 @@
 LN2 = 0.6931471805599453
 LANES = 128
 TILE = 256
-FIRST = 8
-PIECES = 4
+FIRST = 9
+PIECES = 8
 SHARED = 3
 
 MESH = pl.DeviceIdType.MESH

time: 28.9 us -> 28.8 us (level)
  no operation moved by 1% of the time
where the time goes in v7:
time: 28.8 us; the launch traced here: 28.7 us
  Pallas kernels  28 us (97%)
  between operations  0.64 us (2%)
    pallas_call x1, Pallas kernels, local_fit(): pl.pallas_call(functools.partial(em_kernel, sweeps, total_pts, n_half * c...  27.2 us
    pallas_call x1, Pallas kernels, local_fit(): pl.pallas_call(store_kernel, out_shape=tuple((jax.ShapeDtypeStruct(o.shap...  0.83 us

profile of v7, /device:TPU:0, one launch (start us, length us, event | category | flops | bytes accessed | tf_op | source)
XLA Modules:
  0.0 28.7 jit_solution(7542460988909322496)
XLA Ops:
  0.6 27.2 %shard_map.67 = (f32[2,512,128]{2,1,0:T(8,128)S(1)}, f32[2,512]{1,0:T(2,128)S(1)}, f32[2,1024]{1,0:T(2,128)S(1)}) custom-call(f32[3]{0:T(128)} %temp_in.1, bf16[1024,256]{1,0:T(8,128)(2,1)} %x_in.1, f32[2,512,128]{2,1,0:T(8,128)} %mu_in.1, f32[2,512]{1,0:T(2,128)} %lp_in.1), custom_call_target="tpu_custom_call" | custom-call | tf_op jit(solution)/shard_map/pallas_call | solution.py:437
  27.9 0.8 %shard_map.68 = (f32[2,512,128]{2,1,0:T(8,128)}, f32[2,512]{1,0:T(2,128)}, f32[2,1024]{1,0:T(2,128)}) custom-call(f32[2,512,128]{2,1,0:T(8,128)S(1)} %get-tuple-element.6.a, f32[2,512]{1,0:T(2,128)S(1)} %get-tuple-element.7.b, f32[2,1024]{1,0:T(2,128)S(1)} %get-tuple-element.8.c), custom_call_target="tpu_custom_call" | custom-call | tf_op jit(solution)/shard_map/pallas_call | solution.py:478

commit v8 on v7

--- a/solution.py
+++ b/solution.py
@@ -210,8 +210,8 @@
     with jax.named_scope("w_part0"):
         part_copy(0, 0).wait_recv()
     sums = []
-    for p in range(PIECES):
-        at = pl.ds(p * step, step)
+    for p in range(2):
+        at = pl.ds(p * (n_comp // 2), n_comp // 2)
         xsend[at, :] = (part[1, 0, at, :] + inbox[0, 0, at, :]).astype(BF16)
         c = remote(xsend.at[at, :], xin.at[at, :], s_out, r_xs, d_across)
         c.start()

time: 28.8 us -> 28.8 us (level)
  no operation moved by 1% of the time
where the time goes in v8:
time: 28.8 us; the launch traced here: 28.7 us
  Pallas kernels  28.1 us (98%)
  between operations  0.64 us (2%)
    pallas_call x1, Pallas kernels, local_fit(): pl.pallas_call(functools.partial(em_kernel, sweeps, total_pts, n_half * c...  27.2 us
    pallas_call x1, Pallas kernels, local_fit(): pl.pallas_call(store_kernel, out_shape=tuple((jax.ShapeDtypeStruct(o.shap...  0.83 us

profile of v8, /device:TPU:0, one launch (start us, length us, event | category | flops | bytes accessed | tf_op | source)
XLA Modules:
  0.0 28.7 jit_solution(15703671066693832481)
XLA Ops:
  0.6 27.2 %shard_map.67 = (f32[2,512,128]{2,1,0:T(8,128)S(1)}, f32[2,512]{1,0:T(2,128)S(1)}, f32[2,1024]{1,0:T(2,128)S(1)}) custom-call(f32[3]{0:T(128)} %temp_in.1, bf16[1024,256]{1,0:T(8,128)(2,1)} %x_in.1, f32[2,512,128]{2,1,0:T(8,128)} %mu_in.1, f32[2,512]{1,0:T(2,128)} %lp_in.1), custom_call_target="tpu_custom_call" | custom-call | tf_op jit(solution)/shard_map/pallas_call | solution.py:437
  27.9 0.8 %shard_map.68 = (f32[2,512,128]{2,1,0:T(8,128)}, f32[2,512]{1,0:T(2,128)}, f32[2,1024]{1,0:T(2,128)}) custom-call(f32[2,512,128]{2,1,0:T(8,128)S(1)} %get-tuple-element.6.a, f32[2,512]{1,0:T(2,128)S(1)} %get-tuple-element.7.b, f32[2,1024]{1,0:T(2,128)S(1)} %get-tuple-element.8.c), custom_call_target="tpu_custom_call" | custom-call | tf_op jit(solution)/shard_map/pallas_call | solution.py:478
